TPU v7x, 128 devices: a whole 4x4x4 slice. The times are simulated.
128 devices in a mesh: chain: 64 (over z, x_hi, y, core), aux: 2 (over x_lo).
Axes of the slice: x: 4 (x_hi: 2, x_lo: 2; x = x_hi * 2 + x_lo), y: 4, z: 4, core: 2. Of those that a mesh axis runs over, the one named last changes fastest.
Arguments:
- occupied: bfloat16 [8192, 1152], P('chain'), may hold values from -0.1875 to 0.1875
- virtual: bfloat16 [8192, 1152], P('chain'), may hold values from -0.1875 to 0.1875
- three_centre: bfloat16 [32, 8192, 1152], P('aux', 'chain'), may hold values from -6 to 6
- kernel: bfloat16 [32, 32], P('aux'), may hold values from -1 to 1
- profile: int32 [64], replicated, may hold values from 2 to 4
- atom_map: int32 [32], P('aux'), may hold values from 0 to 63
Outputs:
- band_gradient: float32 [8192, 1152], P(('chain', 'aux'))
- polarization: float32 [32, 32], P('aux')
All inputs are finite; a program needn't handle non-finite values.
Results may differ from a plain program's by a relative error of at most 0.0042.
Values may be sent and summed in bfloat16 or wider, within the bound.
A program may use at most 128 MiB of HBM per device.

v0:
```python
import math

import jax
import jax.numpy as jnp
from jax import lax
from jax.sharding import PartitionSpec as P


def passed_along(block, axis, distance):
    devices = range(lax.axis_size(axis))
    route = [(i - distance, i) for i in devices if i - distance in devices]
    return lax.ppermute(block, axis, route)


def from_everyone(shard, axis):
    size = lax.axis_size(axis)
    return lax.all_to_all(
        jnp.broadcast_to(shard[None], (size, *shard.shape)), axis, 0, 0, tiled=True
    )


def taken_together(shard, axis):
    everything = from_everyone(shard, axis)
    return jnp.sum(everything, axis=0)


def cut_along(shard, dim, size):
    before, after = (shard.shape[:dim], shard.shape[dim + 1 :])
    return jnp.moveaxis(shard.reshape(*before, size, -1, *after), dim, 0)


def sent_and_summed(shard, axis, dim):
    parts = cut_along(shard, dim, lax.axis_size(axis))
    arrived = lax.all_to_all(parts, axis, split_axis=0, concat_axis=0, tiled=True)
    return arrived.sum(axis=0)


def shift_blocks(matrix, offset, block_size):
    if offset == 0:
        return matrix
    padding = jnp.zeros(matrix.shape[:-1] + (abs(offset) * block_size,), matrix.dtype)
    if offset > 0:
        return jnp.concatenate([padding, matrix[..., : -offset * block_size]], -1)
    return jnp.concatenate([matrix[..., -offset * block_size :], padding], -1)


def body(occupied, virtual, three_centre, kernel, profile, atom_map):
    block_size = occupied.shape[0]
    band_cols = occupied.shape[1]
    slots_total = band_cols // block_size
    spread = (slots_total - 1) // 2
    nblocks = lax.axis_size("chain")
    position = lax.axis_index("chain")
    slot_ids = jnp.arange(slots_total, dtype=jnp.int32)
    block_ids = jnp.arange(nblocks, dtype=jnp.int32)
    others = position + slot_ids - spread
    neighbours = jnp.sum(jnp.where(block_ids[None, :] == others[:, None], profile[None, :], 0), 1)
    own_width = jnp.sum(jnp.where(block_ids == position, profile, 0))
    allowed = jnp.abs(slot_ids - spread) <= jnp.minimum(own_width, neighbours)
    column_keep = jnp.repeat(allowed, block_size)
    zero_half = jnp.zeros((), jnp.bfloat16)
    occ_masked = jnp.where(column_keep[None, :], occupied, zero_half)
    vir_masked = jnp.where(column_keep[None, :], virtual, zero_half)
    both_bands = jnp.stack([occ_masked, vir_masked])
    fetched = []
    for slot_index in range(slots_total):
        if slot_index == spread:
            fetched.append(both_bands)
        else:
            fetched.append(passed_along(both_bands, "chain", spread - slot_index))
    stack_occ = jnp.concatenate(
        [shift_blocks(fetched[k][0], k - spread, block_size) for k in range(slots_total)], 0
    )
    stack_vir = jnp.concatenate(
        [shift_blocks(fetched[k][1], k - spread, block_size) for k in range(slots_total)], 0
    )
    aux_here = three_centre.shape[0]
    aux_total = kernel.shape[1]
    screen = jnp.abs(atom_map - position) <= nblocks // 4
    local = jnp.where(column_keep[None, None, :] & screen[:, None, None], three_centre, zero_half)
    screened = local.reshape(aux_here * block_size, band_cols)
    coupled = jnp.dot(screened, stack_occ, preferred_element_type=jnp.float32).astype(jnp.bfloat16)
    coupled = coupled.reshape(aux_here, block_size * band_cols)
    partner = jnp.dot(screened, stack_vir, preferred_element_type=jnp.float32).astype(jnp.bfloat16)
    partner = partner.reshape(aux_here, block_size, band_cols)
    piece = lax.all_gather(partner, "aux", axis=0, tiled=True)
    piece_rows = piece.shape[0]
    columns = piece.reshape(piece_rows, block_size * band_cols)
    products = lax.dot_general(
        coupled, columns, (((1,), (1,)), ((), ())), preferred_element_type=jnp.float32
    )
    polar_part = products
    response_sum = jnp.dot(kernel, columns, preferred_element_type=jnp.float32)
    polar_part, response_sum = (polar_part, response_sum)
    polarization = taken_together(polar_part, "chain") * (
        1.0 / math.sqrt(block_size * nblocks * band_cols)
    )
    response = response_sum.astype(jnp.bfloat16).reshape(aux_here * block_size, band_cols)
    partials = lax.dot_general(
        screened, response, (((0,), (0,)), ((), ())), preferred_element_type=jnp.float32
    )
    partials = partials.reshape(slots_total, block_size, band_cols)
    gathered_sum = partials[spread]
    for slot_index in range(slots_total):
        if slot_index != spread:
            moved = shift_blocks(partials[slot_index], spread - slot_index, block_size)
            gathered_sum = gathered_sum + passed_along(
                moved.astype(jnp.bfloat16), "chain", slot_index - spread
            ).astype(moved.dtype)
    gathered_sum = sent_and_summed(gathered_sum, "aux", 0)
    scale_grad = 1.0 / math.sqrt(block_size * aux_total)
    band_gradient = (
        jnp.where(column_keep[None, :], gathered_sum, jnp.zeros((), jnp.float32)) * scale_grad
    )
    return (band_gradient, polarization)


def solution(mesh):
    placed = (
        P("chain", None),
        P("chain", None),
        P("aux", "chain", None),
        P("aux", None),
        P(),
        P("aux"),
    )
    return jax.shard_map(
        body,
        mesh=mesh,
        in_specs=placed,
        out_specs=(P(("chain", "aux"), None), P("aux", None)),
        check_vma=False,
    )
```

profile of v0, /device:TPU:1, one launch (start us, length us, event | category | flops | bytes accessed | tf_op | source)
XLA Modules:
  0.0 339.7 jit_solution(14269273563489841605)
XLA Ops:
  7.2 1.3 fusion.12
  8.5 0.8 select_reduce_fusion
  10.1 1.1 fusion.9
  11.3 5.7 %collective-permute-start = (bf16[2,128,1152]{2,1,0:T(8,128)(2,1)S(1)}, bf16[2,128,1152]{2,1,0:T(8,128)(2,1)S(1)}, u32[]{:S(2)}, u32[]{:S(2)}) collective-permute-start(bf16[2,128,1152]{2,1,0:T(8,128)(2,1)S(1)} %pad_maximum_fusion), channel_id=1, source_target_pairs={{0,8},{2,10},{4,12},{6,14},{8,16},{10,18},{12,20},{14,22},{16,24},... | collective-permute-start | bytes 1769480 | tf_op jit(solution)/shard_map/ppermute | solution.py:12
  17.0 5.3 %collective-permute-start.1 = (bf16[2,128,1152]{2,1,0:T(8,128)(2,1)S(1)}, bf16[2,128,1152]{2,1,0:T(8,128)(2,1)S(1)}, u32[]{:S(2)}, u32[]{:S(2)}) collective-permute-start(bf16[2,128,1152]{2,1,0:T(8,128)(2,1)S(1)} %pad_maximum_fusion), channel_id=1, source_target_pairs={{0,6},{2,8},{4,10},{6,12},{8,14},{10,16},{12,18},{14,20},{16,22},{... | collective-permute-start | bytes 1769480 | tf_op jit(solution)/shard_map/ppermute | solution.py:12
  22.2 3.2 collective-permute-start.2
  25.5 1.9 collective-permute-start.3
  27.4 2.4 collective-permute-start.4
  30.6 2.8 broadcast_select_fusion
  33.4 1.3 collective-permute-start.5
  34.8 6.8 %collective-permute-done.1 = bf16[2,128,1152]{2,1,0:T(8,128)(2,1)S(1)} collective-permute-done((bf16[2,128,1152]{2,1,0:T(8,128)(2,1)S(1)}, bf16[2,128,1152]{2,1,0:T(8,128)(2,1)S(1)}, u32[]{:S(2)}, u32[]{:S(2)}) %collective-permute-start.1) | collective-permute-done | bytes 589856 | tf_op jit(solution)/shard_map/ppermute | solution.py:12
  41.6 1.3 collective-permute-start.6
  43.0 11.3 %collective-permute-done.2 = bf16[2,128,1152]{2,1,0:T(8,128)(2,1)S(1)} collective-permute-done((bf16[2,128,1152]{2,1,0:T(8,128)(2,1)S(1)}, bf16[2,128,1152]{2,1,0:T(8,128)(2,1)S(1)}, u32[]{:S(2)}, u32[]{:S(2)}) %collective-permute-start.2) | collective-permute-done | bytes 589856 | tf_op jit(solution)/shard_map/ppermute | solution.py:12
  54.3 1.3 collective-permute-start.7
  55.6 8.8 %collective-permute-done.3 = bf16[2,128,1152]{2,1,0:T(8,128)(2,1)S(1)} collective-permute-done((bf16[2,128,1152]{2,1,0:T(8,128)(2,1)S(1)}, bf16[2,128,1152]{2,1,0:T(8,128)(2,1)S(1)}, u32[]{:S(2)}, u32[]{:S(2)}) %collective-permute-start.3) | collective-permute-done | bytes 589856 | tf_op jit(solution)/shard_map/ppermute | solution.py:12
  64.5 14.6 %collective-permute-done.6 = bf16[2,128,1152]{2,1,0:T(8,128)(2,1)S(1)} collective-permute-done((bf16[2,128,1152]{2,1,0:T(8,128)(2,1)S(1)}, bf16[2,128,1152]{2,1,0:T(8,128)(2,1)S(1)}, u32[]{:S(2)}, u32[]{:S(2)}) %collective-permute-start.6) | collective-permute-done | bytes 589856 | tf_op jit(solution)/shard_map/ppermute | solution.py:12
  81.0 8.5 %convolution_convert_fusion.2 = bf16[2048,1152]{1,0:T(8,128)(2,1)} fusion(bf16[2048,1152]{1,0:T(8,128)(2,1)S(1)} %bitcast.61, bf16[1152,1152]{1,0:T(8,128)(2,1)S(1)} %pad_dynamic-update-slice_fusion.8), kind=kOutput, calls=%fused_computation.3 | convolution fusion | flops 5438177280 | bytes 12091392 | tf_op jit(solution)/shard_map/dot_general | solution.py:84
  89.6 0.7 pad_dynamic-update-slice_fusion.2
  90.4 0.7 pad_dynamic-update-slice_fusion.1
  91.8 10.9 %convolution_convert_fusion.1 = bf16[2048,1152]{1,0:T(8,128)(2,1)} fusion(bf16[2048,1152]{1,0:T(8,128)(2,1)} %bitcast.62, bf16[1152,1152]{1,0:T(8,128)(2,1)} %pad_dynamic-update-slice_fusion), kind=kOutput, calls=%fused_computation.2 | convolution fusion | flops 5438177280 | bytes 12091392 | tf_op jit(solution)/shard_map/dot_general | solution.py:82
  102.7 5.2 %reshape.85 = bf16[16,147456]{1,0:T(8,128)(2,1)} reshape(bf16[2048,1152]{1,0:T(8,128)(2,1)} %convolution_convert_fusion.1) | data formatting | bytes 9437184 | tf_op jit(solution)/shard_map/reshape | solution.py:83
  107.9 110.5 %all-gather.2.cloned.1.call-done = bf16[32,128,1152]{2,1,0:T(8,128)(2,1)} async-done(((bf16[16,128,1152]{2,1,0:T(8,128)(2,1)}), bf16[32,128,1152]{2,1,0:T(8,128)(2,1)}) %all-gather.2.cloned.1.call-update) | async-done | bytes 9437200 | tf_op jit(solution)/shard_map/all_gather | solution.py:86
  218.4 12.7 %copy.10 = bf16[4,8,128,1152]{3,1,2,0:T(8,128)(2,1)} copy(bf16[4,8,128,1152]{3,2,1,0:T(8,128)(2,1)} %bitcast.59) | data formatting | bytes 18874368
  231.2 7.2 %fusion = bf16[16,147456]{1,0:T(8,128)(2,1)} fusion(bf16[16,32]{1,0:T(8,128)(2,1)S(1)} %copy-done, bf16[32,147456]{1,0:T(8,128)(2,1)} %bitcast.55), kind=kOutput, calls=%fused_computation.1 | convolution fusion | flops 153354240 | bytes 14156800 | tf_op jit(solution)/shard_map/dot_general | solution.py:93
  238.4 5.3 %reshape.83 = bf16[2048,1152]{1,0:T(8,128)(2,1)} reshape(bf16[16,147456]{1,0:T(8,128)(2,1)} %fusion) | data formatting | bytes 9437184 | tf_op jit(solution)/shard_map/reshape | solution.py:98
  243.7 12.6 %fusion.17 = (bf16[1152,1152]{1,0:T(8,128)(2,1)S(1)}, f32[1152,1152]{1,0:T(8,128)}) fusion(bf16[2048,1152]{1,0:T(8,128)(2,1)} %bitcast.63, bf16[2048,1152]{1,0:T(8,128)(2,1)} %reshape.83), kind=kOutput, calls=%fused_computation.67 | convolution fusion | flops 5437145088 | bytes 17399808 | tf_op jit(solution)/shard_map/dot_general | solution.py:99
  256.4 2.7 collective-permute-start.11
  259.2 3.0 collective-permute-start.12
  262.3 1.3 collective-permute-start.10
  263.6 0.7 concatenate.92
  264.3 4.0 %collective-permute-start.13 = (bf16[128,1152]{1,0:T(8,128)(2,1)}, bf16[128,1152]{1,0:T(8,128)(2,1)S(1)}, u32[]{:S(2)}, u32[]{:S(2)}) collective-permute-start(bf16[128,1152]{1,0:T(8,128)(2,1)} %concatenate.92), channel_id=1, source_target_pairs={{0,4},{2,6},{4,8},{6,10},{8,12},{10,14},{12,16},{14,18},{16,20},{1... | collective-permute-start | bytes 884744 | tf_op jit(solution)/shard_map/ppermute | solution.py:12
  268.3 0.7 concatenate.93
  269.1 4.5 %collective-permute-start.14 = (bf16[128,1152]{1,0:T(8,128)(2,1)}, bf16[128,1152]{1,0:T(8,128)(2,1)S(1)}, u32[]{:S(2)}, u32[]{:S(2)}) collective-permute-start(bf16[128,1152]{1,0:T(8,128)(2,1)} %concatenate.93), channel_id=1, source_target_pairs={{0,6},{2,8},{4,10},{6,12},{8,14},{10,16},{12,18},{14,20},{16,22},{... | collective-permute-start | bytes 884744 | tf_op jit(solution)/shard_map/ppermute | solution.py:12
  273.5 0.7 concatenate.88
  274.3 0.7 concatenate.94
  275.0 0.7 concatenate.87
  275.8 1.3 collective-permute-start.9
  277.1 7.3 %collective-permute-start.15 = (bf16[128,1152]{1,0:T(8,128)(2,1)}, bf16[128,1152]{1,0:T(8,128)(2,1)S(1)}, u32[]{:S(2)}, u32[]{:S(2)}) collective-permute-start(bf16[128,1152]{1,0:T(8,128)(2,1)} %concatenate.94), channel_id=1, source_target_pairs={{0,8},{2,10},{4,12},{6,14},{8,16},{10,18},{12,20},{14,22},{16,24},... | collective-permute-start | bytes 884744 | tf_op jit(solution)/shard_map/ppermute | solution.py:12
  284.4 1.3 collective-permute-start.8
  285.8 4.3 %fusion.18 = f32[16,32]{1,0:T(8,128)S(1)} fusion(bf16[16,147456]{1,0:T(8,128)(2,1)} %reshape.85, bf16[32,147456]{1,0:T(8,128)(2,1)S(1)} %bitcast.58), kind=kOutput, calls=%fused_computation.68 | convolution fusion | flops 150994944 | bytes 14157824 | tf_op jit(solution)/shard_map/dot_general | solution.py:89
  290.2 0.9 reshape.86
  291.1 19.2 %all-to-all-start.1 = ((f32[64,1,512]{2,1,0:T(1,128)}), f32[64,1,512]{2,1,0:T(1,128)S(1)}, u32[]{:S(2)}, u32[]{:S(2)}) async-start(f32[64,1,512]{2,1,0:T(1,128)} %reshape.86), calls=%async_computation.1 | async-start | bytes 262144 | tf_op jit(solution)/shard_map/all_to_all | solution.py:17
  310.3 2.2 fusion.7
  312.5 7.8 %all-to-all-done.1 = f32[64,1,512]{2,1,0:T(1,128)S(1)} async-done(((f32[64,1,512]{2,1,0:T(1,128)}), f32[64,1,512]{2,1,0:T(1,128)S(1)}, u32[]{:S(2)}, u32[]{:S(2)}) %all-to-all-start.1) | async-done | bytes 131104 | tf_op jit(solution)/shard_map/all_to_all | solution.py:17
  320.2 3.5 %all-to-all-start = ((f32[2,64,1152]{2,1,0:T(8,128)}), f32[2,64,1152]{2,1,0:T(8,128)S(1)}, u32[]{:S(2)}, u32[]{:S(2)}) async-start(f32[2,64,1152]{2,1,0:T(8,128)} %bitcast.14), calls=%async_computation | async-start | bytes 1179648 | tf_op jit(solution)/shard_map/all_to_all | solution.py:34
  324.3 1.0 reduce
  326.1 6.0 %all-to-all-done = f32[2,64,1152]{2,1,0:T(8,128)S(1)} async-done(((f32[2,64,1152]{2,1,0:T(8,128)}), f32[2,64,1152]{2,1,0:T(8,128)S(1)}, u32[]{:S(2)}, u32[]{:S(2)}) %all-to-all-start) | async-done | bytes 589856 | tf_op jit(solution)/shard_map/all_to_all | solution.py:34
  332.1 0.7 select_multiply_fusion
  (88 shorter events, 5.9 us)
Async XLA Ops:
  7.2 224.0 %copy-start = (bf16[16,32]{1,0:T(8,128)(2,1)S(1)}, bf16[16,32]{1,0:T(8,128)(2,1)}, u32[]{:S(2)}) copy-start(bf16[16,32]{1,0:T(8,128)(2,1)} %param.9) | copy-start | bytes 3076
  7.2 211.3 %all-gather.2.cloned.1.call-start = ((), (), s32[]{:S(2)}) async-start(), calls=%async_computation.2 | async-start | bytes 14155776 | tf_op jit(solution)/shard_map/all_gather | solution.py:86
  11.3 22.1 %collective-permute-start = (bf16[2,128,1152]{2,1,0:T(8,128)(2,1)S(1)}, bf16[2,128,1152]{2,1,0:T(8,128)(2,1)S(1)}, u32[]{:S(2)}, u32[]{:S(2)}) collective-permute-start(bf16[2,128,1152]{2,1,0:T(8,128)(2,1)S(1)} %pad_maximum_fusion), channel_id=1, source_target_pairs={{0,8},{2,10},{4,12},{6,14},{8,16},{10,18},{12,20},{14,22},{16,24},... | collective-permute-start | bytes 1769480 | tf_op jit(solution)/shard_map/ppermute | solution.py:12
  17.0 24.6 %collective-permute-start.1 = (bf16[2,128,1152]{2,1,0:T(8,128)(2,1)S(1)}, bf16[2,128,1152]{2,1,0:T(8,128)(2,1)S(1)}, u32[]{:S(2)}, u32[]{:S(2)}) collective-permute-start(bf16[2,128,1152]{2,1,0:T(8,128)(2,1)S(1)} %pad_maximum_fusion), channel_id=1, source_target_pairs={{0,6},{2,8},{4,10},{6,12},{8,14},{10,16},{12,18},{14,20},{16,22},{... | collective-permute-start | bytes 1769480 | tf_op jit(solution)/shard_map/ppermute | solution.py:12
  22.2 32.0 %collective-permute-start.2 = (bf16[2,128,1152]{2,1,0:T(8,128)(2,1)S(1)}, bf16[2,128,1152]{2,1,0:T(8,128)(2,1)S(1)}, u32[]{:S(2)}, u32[]{:S(2)}) collective-permute-start(bf16[2,128,1152]{2,1,0:T(8,128)(2,1)S(1)} %pad_maximum_fusion), channel_id=1, source_target_pairs={{0,4},{2,6},{4,8},{6,10},{8,12},{10,14},{12,16},{14,18},{16,20},{1... | collective-permute-start | bytes 1769480 | tf_op jit(solution)/shard_map/ppermute | solution.py:12
  25.5 38.9 %collective-permute-start.3 = (bf16[2,128,1152]{2,1,0:T(8,128)(2,1)S(1)}, bf16[2,128,1152]{2,1,0:T(8,128)(2,1)S(1)}, u32[]{:S(2)}, u32[]{:S(2)}) collective-permute-start(bf16[2,128,1152]{2,1,0:T(8,128)(2,1)S(1)} %pad_maximum_fusion), channel_id=1, source_target_pairs={{0,2},{2,4},{4,6},{6,8},{8,10},{10,12},{12,14},{14,16},{16,18},{18... | collective-permute-start | bytes 1769480 | tf_op jit(solution)/shard_map/ppermute | solution.py:12
  27.4 37.0 %collective-permute-start.4 = (bf16[2,128,1152]{2,1,0:T(8,128)(2,1)S(1)}, bf16[2,128,1152]{2,1,0:T(8,128)(2,1)S(1)}, u32[]{:S(2)}, u32[]{:S(2)}) collective-permute-start(bf16[2,128,1152]{2,1,0:T(8,128)(2,1)S(1)} %pad_maximum_fusion), channel_id=1, source_target_pairs={{2,0},{4,2},{6,4},{8,6},{10,8},{12,10},{14,12},{16,14},{18,16},{20... | collective-permute-start | bytes 1769480 | tf_op jit(solution)/shard_map/ppermute | solution.py:12
  33.4 47.6 %copy-start.1 = (bf16[16,128,1152]{2,1,0:T(8,128)(2,1)}, bf16[16,128,1152]{2,1,0:T(8,128)(2,1)S(1)}, u32[]{:S(2)}) copy-start(bf16[16,128,1152]{2,1,0:T(8,128)(2,1)S(1)} %broadcast_select_fusion) | copy-start | bytes 14155780
  33.4 31.0 %collective-permute-start.5 = (bf16[2,128,1152]{2,1,0:T(8,128)(2,1)S(1)}, bf16[2,128,1152]{2,1,0:T(8,128)(2,1)S(1)}, u32[]{:S(2)}, u32[]{:S(2)}) collective-permute-start(bf16[2,128,1152]{2,1,0:T(8,128)(2,1)S(1)} %pad_maximum_fusion), channel_id=1, source_target_pairs={{4,0},{6,2},{8,4},{10,6},{12,8},{14,10},{16,12},{18,14},{20,16},{2... | collective-permute-start | bytes 1769480 | tf_op jit(solution)/shard_map/ppermute | solution.py:12
  41.6 37.6 %collective-permute-start.6 = (bf16[2,128,1152]{2,1,0:T(8,128)(2,1)S(1)}, bf16[2,128,1152]{2,1,0:T(8,128)(2,1)S(1)}, u32[]{:S(2)}, u32[]{:S(2)}) collective-permute-start(bf16[2,128,1152]{2,1,0:T(8,128)(2,1)S(1)} %pad_maximum_fusion), channel_id=1, source_target_pairs={{6,0},{8,2},{10,4},{12,6},{14,8},{16,10},{18,12},{20,14},{22,16},{... | collective-permute-start | bytes 1769480 | tf_op jit(solution)/shard_map/ppermute | solution.py:12
  54.3 25.4 %collective-permute-start.7 = (bf16[2,128,1152]{2,1,0:T(8,128)(2,1)S(1)}, bf16[2,128,1152]{2,1,0:T(8,128)(2,1)S(1)}, u32[]{:S(2)}, u32[]{:S(2)}) collective-permute-start(bf16[2,128,1152]{2,1,0:T(8,128)(2,1)S(1)} %pad_maximum_fusion), channel_id=1, source_target_pairs={{8,0},{10,2},{12,4},{14,6},{16,8},{18,10},{20,12},{22,14},{24,16},... | collective-permute-start | bytes 1769480 | tf_op jit(solution)/shard_map/ppermute | solution.py:12
  79.6 1.0 copy-start.2
  79.6 1.0 copy-start.3
  80.9 8.7 %copy-start.4 = (bf16[1152,1152]{1,0:T(8,128)(2,1)}, bf16[1152,1152]{1,0:T(8,128)(2,1)S(1)}, u32[]{:S(2)}) copy-start(bf16[1152,1152]{1,0:T(8,128)(2,1)S(1)} %get-tuple-element.32) | copy-start | bytes 7962628
  238.4 47.3 %slice-start = ((s8[9437184]{0:T(1024)(128)(4,1)}), s8[1048576]{0:T(1024)(128)(4,1)S(1)}, s32[]{:S(2)}) async-start(s8[9437184]{0:T(1024)(128)(4,1)} %bitcast.56), calls=%async_computation.3 | async-start | bytes 2097152
  243.7 42.1 %slice-start.1 = ((s8[9437184]{0:T(1024)(128)(4,1)}), s8[4194304]{0:T(1024)(128)(4,1)S(1)}, s32[]{:S(2)}) async-start(s8[9437184]{0:T(1024)(128)(4,1)} %bitcast.56), calls=%async_computation.4 | async-start | bytes 8388608
  243.7 42.1 %slice-start.2 = ((s8[9437184]{0:T(1024)(128)(4,1)}), s8[4194304]{0:T(1024)(128)(4,1)S(1)}, s32[]{:S(2)}) async-start(s8[9437184]{0:T(1024)(128)(4,1)} %bitcast.56), calls=%async_computation.5 | async-start | bytes 8388608
  256.4 19.4 %collective-permute-start.11 = (bf16[128,1152]{1,0:T(8,128)(2,1)S(1)}, bf16[128,1152]{1,0:T(8,128)(2,1)S(1)}, u32[]{:S(2)}, u32[]{:S(2)}) collective-permute-start(bf16[128,1152]{1,0:T(8,128)(2,1)S(1)} %concatenate.90), channel_id=1, source_target_pairs={{2,0},{4,2},{6,4},{8,6},{10,8},{12,10},{14,12},{16,14},{18,16},{20... | collective-permute-start | bytes 884744 | tf_op jit(solution)/shard_map/ppermute | solution.py:12
  259.2 17.9 %collective-permute-start.12 = (bf16[128,1152]{1,0:T(8,128)(2,1)S(1)}, bf16[128,1152]{1,0:T(8,128)(2,1)S(1)}, u32[]{:S(2)}, u32[]{:S(2)}) collective-permute-start(bf16[128,1152]{1,0:T(8,128)(2,1)S(1)} %concatenate.91), channel_id=1, source_target_pairs={{0,2},{2,4},{4,6},{6,8},{8,10},{10,12},{12,14},{14,16},{16,18},{18... | collective-permute-start | bytes 884744 | tf_op jit(solution)/shard_map/ppermute | solution.py:12
  262.3 22.2 %collective-permute-start.10 = (bf16[128,1152]{1,0:T(8,128)(2,1)S(1)}, bf16[128,1152]{1,0:T(8,128)(2,1)S(1)}, u32[]{:S(2)}, u32[]{:S(2)}) collective-permute-start(bf16[128,1152]{1,0:T(8,128)(2,1)S(1)} %concatenate.89), channel_id=1, source_target_pairs={{4,0},{6,2},{8,4},{10,6},{12,8},{14,10},{16,12},{18,14},{20,16},{2... | collective-permute-start | bytes 884744 | tf_op jit(solution)/shard_map/ppermute | solution.py:12
  264.3 45.9 %collective-permute-start.13 = (bf16[128,1152]{1,0:T(8,128)(2,1)}, bf16[128,1152]{1,0:T(8,128)(2,1)S(1)}, u32[]{:S(2)}, u32[]{:S(2)}) collective-permute-start(bf16[128,1152]{1,0:T(8,128)(2,1)} %concatenate.92), channel_id=1, source_target_pairs={{0,4},{2,6},{4,8},{6,10},{8,12},{10,14},{12,16},{14,18},{16,20},{1... | collective-permute-start | bytes 884744 | tf_op jit(solution)/shard_map/ppermute | solution.py:12
  269.1 41.2 %collective-permute-start.14 = (bf16[128,1152]{1,0:T(8,128)(2,1)}, bf16[128,1152]{1,0:T(8,128)(2,1)S(1)}, u32[]{:S(2)}, u32[]{:S(2)}) collective-permute-start(bf16[128,1152]{1,0:T(8,128)(2,1)} %concatenate.93), channel_id=1, source_target_pairs={{0,6},{2,8},{4,10},{6,12},{8,14},{10,16},{12,18},{14,20},{16,22},{... | collective-permute-start | bytes 884744 | tf_op jit(solution)/shard_map/ppermute | solution.py:12
  275.8 34.5 %collective-permute-start.9 = (bf16[128,1152]{1,0:T(8,128)(2,1)}, bf16[128,1152]{1,0:T(8,128)(2,1)S(1)}, u32[]{:S(2)}, u32[]{:S(2)}) collective-permute-start(bf16[128,1152]{1,0:T(8,128)(2,1)} %concatenate.88), channel_id=1, source_target_pairs={{6,0},{8,2},{10,4},{12,6},{14,8},{16,10},{18,12},{20,14},{22,16},{... | collective-permute-start | bytes 884744 | tf_op jit(solution)/shard_map/ppermute | solution.py:12
  277.1 33.2 %collective-permute-start.15 = (bf16[128,1152]{1,0:T(8,128)(2,1)}, bf16[128,1152]{1,0:T(8,128)(2,1)S(1)}, u32[]{:S(2)}, u32[]{:S(2)}) collective-permute-start(bf16[128,1152]{1,0:T(8,128)(2,1)} %concatenate.94), channel_id=1, source_target_pairs={{0,8},{2,10},{4,12},{6,14},{8,16},{10,18},{12,20},{14,22},{16,24},... | collective-permute-start | bytes 884744 | tf_op jit(solution)/shard_map/ppermute | solution.py:12
  284.4 25.9 %collective-permute-start.8 = (bf16[128,1152]{1,0:T(8,128)(2,1)}, bf16[128,1152]{1,0:T(8,128)(2,1)S(1)}, u32[]{:S(2)}, u32[]{:S(2)}) collective-permute-start(bf16[128,1152]{1,0:T(8,128)(2,1)} %concatenate.87), channel_id=1, source_target_pairs={{8,0},{10,2},{12,4},{14,6},{16,8},{18,10},{20,12},{22,14},{24,16},... | collective-permute-start | bytes 884744 | tf_op jit(solution)/shard_map/ppermute | solution.py:12
  291.1 29.2 %all-to-all-start.1 = ((f32[64,1,512]{2,1,0:T(1,128)}), f32[64,1,512]{2,1,0:T(1,128)S(1)}, u32[]{:S(2)}, u32[]{:S(2)}) async-start(f32[64,1,512]{2,1,0:T(1,128)} %reshape.86), calls=%async_computation.1 | async-start | bytes 262144 | tf_op jit(solution)/shard_map/all_to_all | solution.py:17
  320.2 11.9 %all-to-all-start = ((f32[2,64,1152]{2,1,0:T(8,128)}), f32[2,64,1152]{2,1,0:T(8,128)S(1)}, u32[]{:S(2)}, u32[]{:S(2)}) async-start(f32[2,64,1152]{2,1,0:T(8,128)} %bitcast.14), calls=%async_computation | async-start | bytes 1179648 | tf_op jit(solution)/shard_map/all_to_all | solution.py:34
Sparse Core Ops, SparseCore 0:
  89.7 128.7 all-gather.1
where the time goes:
time: 341 us; the launch traced here: 340 us
  waiting for transfers between devices  166 us (49%)
  starting transfers between devices  70.5 us (21%)
  matrix products  43.6 us (13%)
  local copies, waits for them, and re-layouts  32.8 us (10%)
  between operations  14.7 us (4%)
  other arithmetic  12.3 us (4%)
    all_gather x1, waiting for transfers between devices, body(): piece = lax.all_gather(partner, 'aux', axis=0, tiled=True)  111 us
    ppermute x16, starting transfers between devices, passed_along(): return lax.ppermute(block, axis, route)  47.8 us
    ppermute x16, waiting for transfers between devices, passed_along(): return lax.ppermute(block, axis, route)  41.6 us
    all_to_all x1, starting transfers between devices, from_everyone(): lax.all_to_all(jnp.broadcast_to(shard[None], (size, *shard.shape)), axis,...  19.2 us
    unnamed x32, local copies, waits for them, and re-layouts  16.4 us
    dot_general x1, matrix products, body(): lax.dot_general(screened, response, (((0,), (0,)), ((), ())), preferred_e...  12.6 us
    dot_general x1, matrix products, body(): jnp.dot(screened, stack_occ, preferred_element_type=jnp.float32)  10.9 us
    dot_general x1, matrix products, body(): jnp.dot(screened, stack_vir, preferred_element_type=jnp.float32)  8.54 us
  transfers between devices with their start and end apart: 19, of which 7 were waited for; matrix products, arithmetic and copies ran while one was open for 11% of the time, Pallas kernels for 0%

commit v1 on v0

v1 whole, which is shorter than its diff:
```python
import functools
import math

import jax
import jax.numpy as jnp
from jax import lax
from jax.experimental import pallas as pl
from jax.experimental.pallas import tpu as pltpu
from jax.sharding import PartitionSpec as P

MESH = pl.DeviceIdType.MESH
BF16 = jnp.bfloat16
F32 = jnp.float32
B = 128
SLOTS = 9
W = SLOTS * B
ROWS = 16
TILES = ((0, 2, 0, 6), (2, 4, 0, 8), (4, 6, 0, 9), (6, 8, 2, 9))

S_IN = 0
UP1, DOWN1, UP2, DOWN2 = 4, 5, 6, 7
PAIR = 8
INFO = 12
GPAIR = 13
GUP2, GDOWN2, GUP1, GDOWN1 = 17, 18, 19, 20
GAUX = 21
POLAR = 22


def kernel(
    nchain,
    naux,
    reach,
    scale_grad,
    scale_pol,
    occ_hbm,
    vir_hbm,
    tc_hbm,
    kern_ref,
    profile_ref,
    atom_ref,
    grad_ref,
    pol_ref,
    s_buf,
    halo,
    pair_halo,
    x_buf,
    v_buf,
    xv_last,
    s_t,
    coupled,
    partner,
    response,
    gram,
    kron,
    info,
    terms,
    pair_out,
    pair_in,
    out2,
    in2,
    out1,
    in1,
    total,
    aux_out,
    aux_in,
    pol_out,
    pol_in,
    send_sem,
    recv_sem,
    local_sem,
):
    half = naux // 2
    chunks = (B // 2) // ROWS
    rounds = int(math.log2(nchain)) + 1
    chips = nchain // 2
    ci = lax.axis_index("chain")
    a = lax.axis_index("aux")
    chip = lax.div(ci, 2)
    core = lax.rem(ci, 2)
    inrow = lax.rem(chip, 4)
    flip_up = lax.div(inrow + 1, 4)
    flip_down = 1 - lax.div(inrow + 3, 4)
    up = (2 * lax.rem(chip + 1, chips) + core, lax.rem(a + flip_up, 2))
    down = (2 * lax.rem(chip + chips - 1, chips) + core, lax.rem(a + flip_down, 2))
    mate = (2 * chip + 1 - core, a)
    twin = (ci, 1 - a)

    def across(bit):
        size = 1 << bit
        return (ci + size * (1 - 2 * lax.rem(lax.div(ci, size), 2)), a)

    polar_peers = [mate, twin] + [across(bit) for bit in range(1, rounds - 1)]

    def remote(src, dst, number, device):
        return pltpu.make_async_remote_copy(
            src_ref=src,
            dst_ref=dst,
            send_sem=send_sem.at[number],
            recv_sem=recv_sem.at[number],
            device_id=device,
            device_id_type=MESH,
        )

    own_copies = [
        pltpu.make_async_copy(occ_hbm, halo.at[2, 0], local_sem.at[0]),
        pltpu.make_async_copy(vir_hbm, halo.at[2, 1], local_sem.at[1]),
    ]
    slab_copies = [
        pltpu.make_async_copy(
            tc_hbm.at[:, chunks * a + g], s_buf.at[g, pl.ds(half * a, half)], local_sem.at[2 + g]
        )
        for g in range(chunks)
    ]
    for copy in own_copies + slab_copies:
        copy.start()

    pair_in[...] = jnp.zeros_like(pair_in)
    row_id = lax.broadcasted_iota(jnp.int32, (half, B), 0)
    screen = jnp.zeros((half, B), F32)
    for p in range(half):
        near = jnp.abs(atom_ref[p] - ci) <= reach
        screen = jnp.where(row_id == p, jnp.where(near, 1.0, 0.0).astype(F32), screen)
    info[a, 0] = jnp.zeros((half, B), F32)
    info[a, 0, :, pl.ds(0, naux)] = kern_ref[...].astype(F32)
    info[a, 1] = screen

    barrier = pltpu.get_barrier_semaphore()
    greeted = [up, down] + polar_peers
    for device in greeted:
        pl.semaphore_signal(barrier, inc=1, device_id=device, device_id_type=MESH)
    pl.semaphore_wait(barrier, len(greeted))

    info_copy = remote(info.at[a], info.at[a], INFO, twin)
    info_copy.start()
    for g in range(chunks):
        remote(
            tc_hbm.at[:, chunks * (1 - a) + g],
            s_buf.at[g, pl.ds(half * a, half)],
            S_IN + g,
            twin,
        ).start()
    for copy in own_copies:
        copy.wait()
    up1 = remote(halo.at[2, :, :, pl.ds(B, 8 * B)], halo.at[1, :, :, pl.ds(B, 8 * B)], UP1, up)
    down1 = remote(halo.at[2, :, :, pl.ds(0, 8 * B)], halo.at[3, :, :, pl.ds(0, 8 * B)], DOWN1, down)
    up1.start()
    down1.start()
    up2 = remote(halo.at[1, :, :, pl.ds(3 * B, 6 * B)], halo.at[0, :, :, pl.ds(3 * B, 6 * B)], UP2, up)
    down2 = remote(halo.at[3, :, :, pl.ds(0, 6 * B)], halo.at[4, :, :, pl.ds(0, 6 * B)], DOWN2, down)
    pair_cols = ((3, 6), (1, 8), (0, 8), (0, 6))
    pair_copies = []
    for q in range(4):
        cols = pl.ds(pair_cols[q][0] * B, pair_cols[q][1] * B)
        pair_copies.append(
            remote(
                halo.at[q + 1 - core, :, :, cols], pair_halo.at[q, :, :, cols], PAIR + q, mate
            )
        )

    gram[...] = jnp.zeros_like(gram)
    terms[...] = jnp.zeros_like(terms)
    x_buf[...] = jnp.zeros_like(x_buf)
    v_buf[...] = jnp.zeros_like(v_buf)

    widths = []
    for t in range(SLOTS):
        block = ci + t - 4
        inside = (block >= 0) & (block < nchain)
        width = profile_ref[jnp.clip(block, 0, nchain - 1)]
        widths.append(jnp.where(inside, width, -1))
    row_ok = [jnp.abs(k - 4) <= jnp.minimum(widths[4], widths[k]) for k in range(SLOTS)]
    keep = [jnp.where(ok, 1.0, 0.0).astype(F32) for ok in row_ok]

    def assemble(d):
        k = d + 4
        for which, target in ((0, x_buf), (1, v_buf)):
            for c in range(max(0, d), min(8, 8 + d) + 1):
                ok = row_ok[k] & (abs(c - k) <= jnp.minimum(widths[k], widths[c]))
                factor = jnp.where(ok, 1.0, 0.0).astype(F32)
                cols = pl.ds((c - d) * B, B)
                if d % 2 == 0:
                    block = halo[2 + d // 2, which, :, cols]
                else:
                    block = pair_halo[(d + 3) // 2, which, :, cols]
                block = (block.astype(F32) * factor).astype(BF16)
                if c == 8:
                    xv_last[pl.ds((k - 4) * B, B), pl.ds(which * B, B)] = block
                else:
                    target[pl.ds(k * B, B), pl.ds(c * B, B)] = block

    assemble(0)
    up1.wait_recv()
    up2.start()
    down1.wait_recv()
    down2.start()
    pair_copies[1].start()
    pair_copies[2].start()

    @pl.when(core == 0)
    def _():
        pair_copies[0].start()

    @pl.when(core == 1)
    def _():
        pair_copies[3].start()

    assemble(-2)
    assemble(2)

    info_copy.wait_recv()
    tall = naux * ROWS
    lane = lax.broadcasted_iota(jnp.int32, (tall, B), 1)
    tall_row = lax.broadcasted_iota(jnp.int32, (tall, B), 0)
    pick = jnp.where(lax.div(tall_row, ROWS) == lane, 1.0, 0.0).astype(F32)
    kern_all = info[:, 0].reshape(naux, B)
    screen_all = info[:, 1].reshape(naux, B)
    screen_tall = jnp.broadcast_to(screen_all[:, None, :], (naux, ROWS, B)).reshape(tall, B)
    kern_tall = jnp.broadcast_to((kern_all * screen_all)[:, None, :], (naux, ROWS, B)).reshape(tall, B)
    spread = lax.dot_general(
        kern_tall.astype(BF16),
        (pick * screen_tall).astype(BF16),
        (((1,), (1,)), ((), ())),
        preferred_element_type=F32,
    )
    same_row = lax.rem(lax.broadcasted_iota(jnp.int32, (tall, tall), 0), ROWS) == lax.rem(
        lax.broadcasted_iota(jnp.int32, (tall, tall), 1), ROWS
    )
    kron[...] = jnp.where(same_row, spread, 0.0).astype(BF16)

    up2.wait_recv()
    down2.wait_recv()

    @pl.when(core == 1)
    def _():
        pair_copies[0].start()

    @pl.when(core == 0)
    def _():
        pair_copies[3].start()

    assemble(-4)
    assemble(4)
    for q, d in ((1, -1), (2, 1), (0, -3), (3, 3)):
        pair_copies[q].wait_recv()
        assemble(d)

    def arrived(g):
        pltpu.make_async_copy(
            tc_hbm.at[:, chunks * a + g], s_buf.at[g, pl.ds(half * a, half)], local_sem.at[2 + g]
        ).wait()
        remote(
            tc_hbm.at[:, chunks * (1 - a) + g],
            s_buf.at[g, pl.ds(half * (1 - a), half)],
            S_IN + g,
            twin,
        ).wait_recv()

    def step(g, carry):
        arrived(g)

        def cut(k0, k1):
            return s_buf[g, :, :, pl.ds(k0 * B, (k1 - k0) * B)].reshape(tall, (k1 - k0) * B)

        for c0, c1, k0, k1 in TILES:
            cols = pl.ds(c0 * B, (c1 - c0) * B)
            rows = pl.ds(k0 * B, (k1 - k0) * B)
            coupled[:, cols] = jnp.dot(cut(k0, k1), x_buf[rows, cols], preferred_element_type=F32).astype(BF16)
            partner[:, cols] = jnp.dot(cut(k0, k1), v_buf[rows, cols], preferred_element_type=F32).astype(BF16)
        last = jnp.dot(cut(4, 9), xv_last[...], preferred_element_type=F32).astype(BF16)
        coupled[:, pl.ds(8 * B, B)] = last[:, :B]
        partner[:, pl.ds(8 * B, B)] = last[:, B:]
        gram[...] += lax.dot_general(
            coupled[...], partner[...], (((1,), (1,)), ((), ())), preferred_element_type=F32
        )
        response[...] = jnp.dot(kron[...], partner[...], preferred_element_type=F32).astype(BF16)
        s_t[...] = cut(0, 9).T
        for c0, c1, k0, k1 in TILES + ((8, 9, 4, 9),):
            cols = pl.ds(c0 * B, (c1 - c0) * B)
            rows = pl.ds(k0 * B, (k1 - k0) * B)
            terms[rows, cols] += jnp.dot(s_t[rows, :], response[:, cols], preferred_element_type=F32)
        return carry

    lax.fori_loop(0, chunks, step, 0)

    def own_terms(d, cj0, cj1):
        k = d + 4
        return terms[pl.ds(k * B, B), pl.ds((cj0 + d) * B, (cj1 - cj0) * B)] * keep[k]

    gpair = []
    for q, d in enumerate((-3, -1, 1, 3)):
        c0, n = pair_cols[q]
        cols = pl.ds(c0 * B, n * B)
        pair_out[q, :, cols] = own_terms(d, c0, c0 + n).astype(BF16)
        copy = remote(pair_out.at[q, :, cols], pair_in.at[q + core, :, cols], GPAIR + q, mate)
        copy.start()
        gpair.append(copy)

    folded = jnp.where(same_row, gram[...], 0.0).reshape(naux, ROWS, tall).sum(1)
    polar = jnp.dot(folded, pick, preferred_element_type=F32, precision=lax.Precision.HIGHEST)
    square_row = lax.broadcasted_iota(jnp.int32, (naux, B), 0)
    square_lane = lax.broadcasted_iota(jnp.int32, (naux, B), 1)
    screen_lane = jnp.sum(jnp.where(square_row == square_lane, screen_all, 0.0), axis=0, keepdims=True)
    polar = polar * screen_all * screen_lane
    pol_out[0] = polar
    pol_copies = [
        remote(pol_out.at[r], pol_in.at[r], POLAR + r, polar_peers[r]) for r in range(rounds)
    ]
    pol_copies[0].start()

    def polar_round(r):
        pol_copies[r].wait_recv()
        pol_out[r + 1] = pol_out[r] + pol_in[r]
        if r + 1 < rounds:
            pol_copies[r + 1].start()

    for copy in gpair:
        copy.wait_recv()
    out2[0] = jnp.concatenate(
        [
            own_terms(4, 0, 5) + pair_in[4, :, pl.ds(0, 5 * B)].astype(F32),
            pair_in[4, :, pl.ds(5 * B, B)].astype(F32),
        ],
        axis=1,
    ).astype(BF16)
    gup2 = remote(out2.at[0], in2.at[0], GUP2, up)
    gup2.start()
    out2[1] = jnp.concatenate(
        [
            pair_in[0, :, pl.ds(3 * B, B)].astype(F32),
            own_terms(-4, 4, 9) + pair_in[0, :, pl.ds(4 * B, 5 * B)].astype(F32),
        ],
        axis=1,
    ).astype(BF16)
    gdown2 = remote(out2.at[1], in2.at[1], GDOWN2, down)
    gdown2.start()
    polar_round(0)
    polar_round(1)

    gup2.wait_recv()
    for c in range(8):
        cols = pl.ds(c * B, B)
        part = pair_in[3, :, cols].astype(F32)
        if c < 7:
            part = part + own_terms(2, c, c + 1)
        if c < 6:
            part = part + in2[0, :, cols].astype(F32)
        out1[0, :, cols] = part.astype(BF16)
    gup1 = remote(out1.at[0], in1.at[0], GUP1, up)
    gup1.start()
    gdown2.wait_recv()
    for c in range(8):
        cols = pl.ds(c * B, B)
        part = pair_in[1, :, pl.ds((c + 1) * B, B)].astype(F32)
        if c >= 1:
            part = part + own_terms(-2, c + 1, c + 2)
        if c >= 2:
            part = part + in2[1, :, pl.ds((c - 2) * B, B)].astype(F32)
        out1[1, :, cols] = part.astype(BF16)
    gdown1 = remote(out1.at[1], in1.at[1], GDOWN1, down)
    gdown1.start()
    for r in range(2, rounds):
        polar_round(r)
    pol_ref[...] = pol_out[rounds, pl.ds(half * a, half), pl.ds(0, naux)] * scale_pol

    total[...] = terms[pl.ds(4 * B, B), :] + pair_in[2].astype(F32)
    gup1.wait_recv()
    total[:, pl.ds(0, 8 * B)] += in1[0].astype(F32)
    gdown1.wait_recv()
    total[:, pl.ds(B, 8 * B)] += in1[1].astype(F32)
    rows = B // 2
    aux_out[...] = total[pl.ds(rows * (1 - a), rows), :].astype(BF16)
    gaux = remote(aux_out, aux_in, GAUX, twin)
    gaux.start()
    gaux.wait_recv()
    for c in range(SLOTS):
        cols = pl.ds(c * B, B)
        grad_ref[:, cols] = (
            total[pl.ds(rows * a, rows), cols] + aux_in[:, cols].astype(F32)
        ) * (keep[c] * scale_grad)

    info_copy.wait_send()
    for g in range(chunks):
        remote(
            tc_hbm.at[:, chunks * (1 - a) + g],
            s_buf.at[g, pl.ds(half * a, half)],
            S_IN + g,
            twin,
        ).wait_send()
    for copy in [up1, down1, up2, down2] + pair_copies + gpair + [gup2, gdown2, gup1, gdown1, gaux] + pol_copies:
        copy.wait_send()


def body(occupied, virtual, three_centre, kern, profile, atom_map):
    nchain = lax.axis_size("chain")
    half = three_centre.shape[0]
    naux = kern.shape[1]
    chunks = (B // 2) // ROWS
    tall = naux * ROWS
    rounds = int(math.log2(nchain)) + 1
    slabs = three_centre.reshape(half, B // ROWS, ROWS, W)
    anyspace = pl.BlockSpec(memory_space=pl.ANY)
    vmem = pl.BlockSpec(memory_space=pltpu.VMEM)
    smem = pl.BlockSpec(memory_space=pltpu.SMEM)
    grad, pol = pl.pallas_call(
        functools.partial(
            kernel,
            nchain,
            naux,
            nchain // 4,
            1.0 / math.sqrt(B * naux),
            1.0 / math.sqrt(B * nchain * W),
        ),
        out_shape=(
            jax.ShapeDtypeStruct((B // 2, W), F32),
            jax.ShapeDtypeStruct((half, naux), F32),
        ),
        in_specs=[anyspace, anyspace, anyspace, vmem, smem, smem],
        out_specs=(vmem, vmem),
        scratch_shapes=[
            pltpu.VMEM((chunks, naux, ROWS, W), BF16),
            pltpu.VMEM((5, 2, B, W), BF16),
            pltpu.VMEM((4, 2, B, W), BF16),
            pltpu.VMEM((W, W), BF16),
            pltpu.VMEM((W, W), BF16),
            pltpu.VMEM((5 * B, 2 * B), BF16),
            pltpu.VMEM((W, tall), BF16),
            pltpu.VMEM((tall, W), BF16),
            pltpu.VMEM((tall, W), BF16),
            pltpu.VMEM((tall, W), BF16),
            pltpu.VMEM((tall, tall), F32),
            pltpu.VMEM((tall, tall), BF16),
            pltpu.VMEM((2, 2, half, B), F32),
            pltpu.VMEM((W, W), F32),
            pltpu.VMEM((4, B, W), BF16),
            pltpu.VMEM((5, B, W), BF16),
            pltpu.VMEM((2, B, 6 * B), BF16),
            pltpu.VMEM((2, B, 6 * B), BF16),
            pltpu.VMEM((2, B, 8 * B), BF16),
            pltpu.VMEM((2, B, 8 * B), BF16),
            pltpu.VMEM((B, W), F32),
            pltpu.VMEM((B // 2, W), BF16),
            pltpu.VMEM((B // 2, W), BF16),
            pltpu.VMEM((rounds + 1, naux, B), F32),
            pltpu.VMEM((rounds, naux, B), F32),
            pltpu.SemaphoreType.DMA((POLAR + rounds,)),
            pltpu.SemaphoreType.DMA((POLAR + rounds,)),
            pltpu.SemaphoreType.DMA((2 + chunks,)),
        ],
        compiler_params=pltpu.CompilerParams(
            collective_id=0, has_side_effects=True, vmem_limit_bytes=60 * 2**20
        ),
        name="rpa",
    )(occupied, virtual, slabs, kern, profile, atom_map)
    return grad, pol


def solution(mesh):
    placed = (
        P("chain", None),
        P("chain", None),
        P("aux", "chain", None),
        P("aux", None),
        P(),
        P("aux"),
    )
    return jax.shard_map(
        body,
        mesh=mesh,
        in_specs=placed,
        out_specs=(P(("chain", "aux"), None), P("aux", None)),
        check_vma=False,
    )
```

time: 341 us -> 104 us (0.30)
  the two profiles are of different devices: /device:TPU:1 before, /device:TPU:10 now
where the time goes in v1:
time: 104 us
  Pallas kernels  100 us (96%)
  local copies, waits for them, and re-layouts  2.99 us (3%)
    pallas_call x1, Pallas kernels, body(): pl.pallas_call(functools.partial(kernel, nchain, naux, nchain // 4, 1.0 /...  100 us
    unnamed x2, local copies, waits for them, and re-layouts  2.99 us

profile of v1, /device:TPU:10, one launch (start us, length us, event | category | flops | bytes accessed | tf_op | source)
XLA Modules:
  0.0 103.9 jit_solution(17701115951127993170)
XLA Ops:
  0.6 100.2 %rpa.1 = (f32[64,1152]{1,0:T(8,128)}, f32[16,32]{1,0:T(8,128)}) custom-call(bf16[128,1152]{1,0:T(8,128)(2,1)} %occ_hbm.1, bf16[128,1152]{1,0:T(8,128)(2,1)} %vir_hbm.1, bf16[16,8,16,1152]{3,2,1,0:T(8,128)(2,1)} %bitcast.1, bf16[16,32]{1,0:T(8,128)(2,1)} %kern_ref.1, s32[64]{0:T(128)} %profile_ref.1, s32[16]{0:T(128)} %atom_ref.1), custom_call_target="tpu_custom_call" | custom-call | tf_op jit(solution)/shard_map/rpa/pallas_call | solution.py:405
  100.9 1.7 %copy.10 = f32[64,1152]{1,0:T(8,128)} copy(f32[64,1152]{1,0:T(8,128)} %get-tuple-element.4) | data formatting | bytes 589824
  102.6 1.3 %copy.11 = f32[16,32]{1,0:T(8,128)} copy(f32[16,32]{1,0:T(8,128)} %get-tuple-element.5) | data formatting | bytes 4096

commit v2 on v1

--- a/solution.py
+++ b/solution.py
@@ -22,9 +22,11 @@
 PAIR = 8
 INFO = 12
 GPAIR = 13
-GUP2, GDOWN2, GUP1, GDOWN1 = 17, 18, 19, 20
-GAUX = 21
-POLAR = 22
+GUP2, GDOWN2, GUP1, GDOWN1, GAUX = 21, 23, 25, 27, 29
+POLAR = 31
+PIECES = 2
+RUN = B // 4
+VMEM_LIMIT = 60 * 2**20
 
 
 def kernel(
@@ -36,9 +38,9 @@
     occ_hbm,
     vir_hbm,
     tc_hbm,
-    kern_ref,
-    profile_ref,
-    atom_ref,
+    kern_hbm,
+    profile_hbm,
+    atom_hbm,
     grad_ref,
     pol_ref,
     s_buf,
@@ -66,13 +68,15 @@
     aux_in,
     pol_out,
     pol_in,
+    kern_ref,
+    profile_ref,
+    atom_ref,
     send_sem,
     recv_sem,
     local_sem,
 ):
     half = naux // 2
     chunks = (B // 2) // ROWS
-    rounds = int(math.log2(nchain)) + 1
     chips = nchain // 2
     ci = lax.axis_index("chain")
     a = lax.axis_index("aux")
@@ -90,7 +94,21 @@
         size = 1 << bit
         return (ci + size * (1 - 2 * lax.rem(lax.div(ci, size), 2)), a)
 
-    polar_peers = [mate, twin] + [across(bit) for bit in range(1, rounds - 1)]
+    def xor(low, value):
+        device = ci
+        for bit in (0, 1):
+            if value >> bit & 1:
+                size = 1 << (low + bit)
+                device = device + size * (1 - 2 * lax.rem(lax.div(ci, size), 2))
+        return (device, a)
+
+    groups = [[mate], [twin]]
+    if nchain >= 64:
+        groups.append([xor(4, v) for v in (1, 2, 3)])
+    if nchain >= 16:
+        groups.append([xor(3, 1)])
+    groups.append([xor(1, v) for v in (1, 2, 3)])
+    polar_peers = [device for group in groups for device in group]
 
     def remote(src, dst, number, device):
         return pltpu.make_async_remote_copy(
@@ -112,10 +130,24 @@
         )
         for g in range(chunks)
     ]
-    for copy in own_copies + slab_copies:
+    table_copies = [
+        pltpu.make_async_copy(src, dst, local_sem.at[2 + chunks + n])
+        for n, (src, dst) in enumerate(
+            ((kern_hbm, kern_ref), (profile_hbm, profile_ref), (atom_hbm, atom_ref))
+        )
+    ]
+
+    for slot, c0, n in ((0, 3, 6), (1, 1, 2), (2, 0, 1), (2, 8, 1), (3, 6, 2), (4, 0, 6)):
+        pair_in[slot, :, pl.ds(c0 * B, n * B)] = jnp.zeros((B, n * B), BF16)
+
+    barrier = pltpu.get_barrier_semaphore()
+    greeted = [up, down] + polar_peers
+    for device in greeted:
+        pl.semaphore_signal(barrier, inc=1, device_id=device, device_id_type=MESH)
+    for copy in own_copies + table_copies + slab_copies:
         copy.start()
-
-    pair_in[...] = jnp.zeros_like(pair_in)
+    for copy in table_copies:
+        copy.wait()
     row_id = lax.broadcasted_iota(jnp.int32, (half, B), 0)
     screen = jnp.zeros((half, B), F32)
     for p in range(half):
@@ -124,15 +156,9 @@
     info[a, 0] = jnp.zeros((half, B), F32)
     info[a, 0, :, pl.ds(0, naux)] = kern_ref[...].astype(F32)
     info[a, 1] = screen
-
-    barrier = pltpu.get_barrier_semaphore()
-    greeted = [up, down] + polar_peers
-    for device in greeted:
-        pl.semaphore_signal(barrier, inc=1, device_id=device, device_id_type=MESH)
     pl.semaphore_wait(barrier, len(greeted))
 
     info_copy = remote(info.at[a], info.at[a], INFO, twin)
-    info_copy.start()
     for g in range(chunks):
         remote(
             tc_hbm.at[:, chunks * (1 - a) + g],
@@ -140,6 +166,8 @@
             S_IN + g,
             twin,
         ).start()
+        if g == 0:
+            info_copy.start()
     for copy in own_copies:
         copy.wait()
     up1 = remote(halo.at[2, :, :, pl.ds(B, 8 * B)], halo.at[1, :, :, pl.ds(B, 8 * B)], UP1, up)
@@ -159,6 +187,8 @@
         )
 
     gram[...] = jnp.zeros_like(gram)
+    coupled[...] = jnp.zeros_like(coupled)
+    partner[...] = jnp.zeros_like(partner)
     terms[...] = jnp.zeros_like(terms)
     x_buf[...] = jnp.zeros_like(x_buf)
     v_buf[...] = jnp.zeros_like(v_buf)
@@ -245,36 +275,43 @@
         pair_copies[q].wait_recv()
         assemble(d)
 
-    def arrived(g):
+    def add_gram():
+        gram[...] += lax.dot_general(
+            coupled[...], partner[...], (((1,), (1,)), ((), ())), preferred_element_type=F32
+        )
+
+    def products(g, slab):
+        mine = pl.ds(half * slab, half)
+        short = half * ROWS
+        tall_rows = pl.ds(pl.multiple_of(short * slab, short), short)
+
+        def cut(k0, k1):
+            return s_buf[g, mine, :, pl.ds(k0 * B, (k1 - k0) * B)].reshape(short, (k1 - k0) * B)
+
+        for c0, c1, k0, k1 in TILES:
+            cols = pl.ds(c0 * B, (c1 - c0) * B)
+            rows = pl.ds(k0 * B, (k1 - k0) * B)
+            coupled[tall_rows, cols] = jnp.dot(cut(k0, k1), x_buf[rows, cols], preferred_element_type=F32).astype(BF16)
+            partner[tall_rows, cols] = jnp.dot(cut(k0, k1), v_buf[rows, cols], preferred_element_type=F32).astype(BF16)
+        last = jnp.dot(cut(4, 9), xv_last[...], preferred_element_type=F32).astype(BF16)
+        coupled[tall_rows, pl.ds(8 * B, B)] = last[:, :B]
+        partner[tall_rows, pl.ds(8 * B, B)] = last[:, B:]
+
+    def step(g, carry):
         pltpu.make_async_copy(
             tc_hbm.at[:, chunks * a + g], s_buf.at[g, pl.ds(half * a, half)], local_sem.at[2 + g]
         ).wait()
+        products(g, a)
         remote(
             tc_hbm.at[:, chunks * (1 - a) + g],
             s_buf.at[g, pl.ds(half * (1 - a), half)],
             S_IN + g,
             twin,
         ).wait_recv()
-
-    def step(g, carry):
-        arrived(g)
-
-        def cut(k0, k1):
-            return s_buf[g, :, :, pl.ds(k0 * B, (k1 - k0) * B)].reshape(tall, (k1 - k0) * B)
-
-        for c0, c1, k0, k1 in TILES:
-            cols = pl.ds(c0 * B, (c1 - c0) * B)
-            rows = pl.ds(k0 * B, (k1 - k0) * B)
-            coupled[:, cols] = jnp.dot(cut(k0, k1), x_buf[rows, cols], preferred_element_type=F32).astype(BF16)
-            partner[:, cols] = jnp.dot(cut(k0, k1), v_buf[rows, cols], preferred_element_type=F32).astype(BF16)
-        last = jnp.dot(cut(4, 9), xv_last[...], preferred_element_type=F32).astype(BF16)
-        coupled[:, pl.ds(8 * B, B)] = last[:, :B]
-        partner[:, pl.ds(8 * B, B)] = last[:, B:]
-        gram[...] += lax.dot_general(
-            coupled[...], partner[...], (((1,), (1,)), ((), ())), preferred_element_type=F32
-        )
+        products(g, 1 - a)
+        add_gram()
         response[...] = jnp.dot(kron[...], partner[...], preferred_element_type=F32).astype(BF16)
-        s_t[...] = cut(0, 9).T
+        s_t[...] = s_buf[g].reshape(tall, W).T
         for c0, c1, k0, k1 in TILES + ((8, 9, 4, 9),):
             cols = pl.ds(c0 * B, (c1 - c0) * B)
             rows = pl.ds(k0 * B, (k1 - k0) * B)
@@ -283,101 +320,144 @@
 
     lax.fori_loop(0, chunks, step, 0)
 
-    def own_terms(d, cj0, cj1):
+    def own_terms(p, run, d, cj, n=1):
         k = d + 4
-        return terms[pl.ds(k * B, B), pl.ds((cj0 + d) * B, (cj1 - cj0) * B)] * keep[k]
-
-    gpair = []
-    for q, d in enumerate((-3, -1, 1, 3)):
-        c0, n = pair_cols[q]
-        cols = pl.ds(c0 * B, n * B)
-        pair_out[q, :, cols] = own_terms(d, c0, c0 + n).astype(BF16)
-        copy = remote(pair_out.at[q, :, cols], pair_in.at[q + core, :, cols], GPAIR + q, mate)
-        copy.start()
-        gpair.append(copy)
+        return terms[pl.ds(k * B + run * 2 * RUN + p * RUN, RUN), pl.ds((cj + d) * B, n * B)] * keep[k]
+
+    def mates(p, run, slot, cj):
+        return pair_in[slot, pl.ds((2 * p + run) * RUN, RUN), pl.ds(cj * B, B)].astype(F32)
+
+    def piece(p):
+        return pl.ds(2 * p * RUN, 2 * RUN)
+
+    gpair = [[None] * 4 for _ in range(PIECES)]
+    for p in range(PIECES):
+        for q in (0, 3, 1, 2):
+            c0, n = pair_cols[q]
+            cols = pl.ds(c0 * B, n * B)
+            for run in (0, 1):
+                pair_out[q, pl.ds((2 * p + run) * RUN, RUN), cols] = own_terms(p, run, 2 * q - 3, c0, n).astype(BF16)
+            gpair[p][q] = remote(
+                pair_out.at[q, piece(p), cols],
+                pair_in.at[q + core, piece(p), cols],
+                GPAIR + 4 * p + q,
+                mate,
+            )
+            gpair[p][q].start()
+
+    gup2, gdown2, gup1, gdown1, gaux = [], [], [], [], []
+    for p in range(PIECES):
+        for q in (0, 3, 1, 2):
+            gpair[p][q].wait_recv()
+        for run in (0, 1):
+            at = pl.ds((2 * p + run) * RUN, RUN)
+            for c in range(6):
+                part = mates(p, run, 4, c)
+                if c < 5:
+                    part = part + own_terms(p, run, 4, c)
+                out2[0, at, pl.ds(c * B, B)] = part.astype(BF16)
+        gup2.append(remote(out2.at[0, piece(p)], in2.at[0, piece(p)], GUP2 + p, up))
+        gup2[p].start()
+        for run in (0, 1):
+            at = pl.ds((2 * p + run) * RUN, RUN)
+            for c in range(6):
+                part = mates(p, run, 0, c + 3)
+                if c >= 1:
+                    part = part + own_terms(p, run, -4, c + 3)
+                out2[1, at, pl.ds(c * B, B)] = part.astype(BF16)
+        gdown2.append(remote(out2.at[1, piece(p)], in2.at[1, piece(p)], GDOWN2 + p, down))
+        gdown2[p].start()
 
     folded = jnp.where(same_row, gram[...], 0.0).reshape(naux, ROWS, tall).sum(1)
     polar = jnp.dot(folded, pick, preferred_element_type=F32, precision=lax.Precision.HIGHEST)
     square_row = lax.broadcasted_iota(jnp.int32, (naux, B), 0)
     square_lane = lax.broadcasted_iota(jnp.int32, (naux, B), 1)
     screen_lane = jnp.sum(jnp.where(square_row == square_lane, screen_all, 0.0), axis=0, keepdims=True)
-    polar = polar * screen_all * screen_lane
-    pol_out[0] = polar
-    pol_copies = [
-        remote(pol_out.at[r], pol_in.at[r], POLAR + r, polar_peers[r]) for r in range(rounds)
-    ]
-    pol_copies[0].start()
+    pol_out[0] = polar * screen_all * screen_lane
+    pol_copies = []
+    for r, group in enumerate(groups):
+        first = sum(len(g) for g in groups[:r])
+        pol_copies.append(
+            [
+                remote(pol_out.at[r], pol_in.at[first + n], POLAR + first + n, device)
+                for n, device in enumerate(group)
+            ]
+        )
+
+    def polar_start(r):
+        for copy in pol_copies[r]:
+            copy.start()
 
     def polar_round(r):
-        pol_copies[r].wait_recv()
-        pol_out[r + 1] = pol_out[r] + pol_in[r]
-        if r + 1 < rounds:
-            pol_copies[r + 1].start()
-
-    for copy in gpair:
-        copy.wait_recv()
-    out2[0] = jnp.concatenate(
-        [
-            own_terms(4, 0, 5) + pair_in[4, :, pl.ds(0, 5 * B)].astype(F32),
-            pair_in[4, :, pl.ds(5 * B, B)].astype(F32),
-        ],
-        axis=1,
-    ).astype(BF16)
-    gup2 = remote(out2.at[0], in2.at[0], GUP2, up)
-    gup2.start()
-    out2[1] = jnp.concatenate(
-        [
-            pair_in[0, :, pl.ds(3 * B, B)].astype(F32),
-            own_terms(-4, 4, 9) + pair_in[0, :, pl.ds(4 * B, 5 * B)].astype(F32),
-        ],
-        axis=1,
-    ).astype(BF16)
-    gdown2 = remote(out2.at[1], in2.at[1], GDOWN2, down)
-    gdown2.start()
+        for copy in pol_copies[r]:
+            copy.wait_recv()
+        first = sum(len(g) for g in groups[:r])
+        value = pol_out[r] + pol_in[first]
+        if len(groups[r]) == 3:
+            value = value + (pol_in[first + 1] + pol_in[first + 2])
+        pol_out[r + 1] = value
+        if r + 1 < len(groups):
+            polar_start(r + 1)
+
+    polar_start(0)
     polar_round(0)
-    polar_round(1)
-
-    gup2.wait_recv()
-    for c in range(8):
-        cols = pl.ds(c * B, B)
-        part = pair_in[3, :, cols].astype(F32)
-        if c < 7:
-            part = part + own_terms(2, c, c + 1)
-        if c < 6:
-            part = part + in2[0, :, cols].astype(F32)
-        out1[0, :, cols] = part.astype(BF16)
-    gup1 = remote(out1.at[0], in1.at[0], GUP1, up)
-    gup1.start()
-    gdown2.wait_recv()
-    for c in range(8):
-        cols = pl.ds(c * B, B)
-        part = pair_in[1, :, pl.ds((c + 1) * B, B)].astype(F32)
-        if c >= 1:
-            part = part + own_terms(-2, c + 1, c + 2)
-        if c >= 2:
-            part = part + in2[1, :, pl.ds((c - 2) * B, B)].astype(F32)
-        out1[1, :, cols] = part.astype(BF16)
-    gdown1 = remote(out1.at[1], in1.at[1], GDOWN1, down)
-    gdown1.start()
-    for r in range(2, rounds):
+    for p in range(PIECES):
+        gup2[p].wait_recv()
+        for run in (0, 1):
+            at = pl.ds((2 * p + run) * RUN, RUN)
+            for c in range(8):
+                part = mates(p, run, 3, c)
+                if c < 7:
+                    part = part + own_terms(p, run, 2, c)
+                if c < 6:
+                    part = part + in2[0, at, pl.ds(c * B, B)].astype(F32)
+                out1[0, at, pl.ds(c * B, B)] = part.astype(BF16)
+        gup1.append(remote(out1.at[0, piece(p)], in1.at[0, piece(p)], GUP1 + p, up))
+        gup1[p].start()
+        gdown2[p].wait_recv()
+        for run in (0, 1):
+            at = pl.ds((2 * p + run) * RUN, RUN)
+            for c in range(8):
+                part = mates(p, run, 1, c + 1)
+                if c >= 1:
+                    part = part + own_terms(p, run, -2, c + 1)
+                if c >= 2:
+                    part = part + in2[1, at, pl.ds((c - 2) * B, B)].astype(F32)
+                out1[1, at, pl.ds(c * B, B)] = part.astype(BF16)
+        gdown1.append(remote(out1.at[1, piece(p)], in1.at[1, piece(p)], GDOWN1 + p, down))
+        gdown1[p].start()
+        if p + 1 < len(groups) - 1:
+            polar_round(p + 1)
+    for p in range(PIECES):
+        gup1[p].wait_recv()
+        gdown1[p].wait_recv()
+        for run in (0, 1):
+            at = pl.ds((2 * p + run) * RUN, RUN)
+            for c in range(SLOTS):
+                part = mates(p, run, 2, c) + own_terms(p, run, 0, c)
+                if c < 8:
+                    part = part + in1[0, at, pl.ds(c * B, B)].astype(F32)
+                if c >= 1:
+                    part = part + in1[1, at, pl.ds((c - 1) * B, B)].astype(F32)
+                total[run, pl.ds(p * RUN, RUN), pl.ds(c * B, B)] = part
+        there = pl.ds(p * RUN, RUN)
+        aux_out[there, :] = total[1 - a, there, :].astype(BF16)
+        gaux.append(remote(aux_out.at[there], aux_in.at[there], GAUX + p, twin))
+        gaux[p].start()
+        if p + PIECES + 1 < len(groups) - 1:
+            polar_round(p + PIECES + 1)
+    for r in range(min(2 * PIECES + 1, len(groups) - 1), len(groups) - 1):
         polar_round(r)
-    pol_ref[...] = pol_out[rounds, pl.ds(half * a, half), pl.ds(0, naux)] * scale_pol
-
-    total[...] = terms[pl.ds(4 * B, B), :] + pair_in[2].astype(F32)
-    gup1.wait_recv()
-    total[:, pl.ds(0, 8 * B)] += in1[0].astype(F32)
-    gdown1.wait_recv()
-    total[:, pl.ds(B, 8 * B)] += in1[1].astype(F32)
-    rows = B // 2
-    aux_out[...] = total[pl.ds(rows * (1 - a), rows), :].astype(BF16)
-    gaux = remote(aux_out, aux_in, GAUX, twin)
-    gaux.start()
-    gaux.wait_recv()
-    for c in range(SLOTS):
-        cols = pl.ds(c * B, B)
-        grad_ref[:, cols] = (
-            total[pl.ds(rows * a, rows), cols] + aux_in[:, cols].astype(F32)
-        ) * (keep[c] * scale_grad)
+    for p in range(PIECES):
+        gaux[p].wait_recv()
+        there = pl.ds(p * RUN, RUN)
+        for c in range(SLOTS):
+            cols = pl.ds(c * B, B)
+            grad_ref[there, cols] = (
+                total[a, there, cols] + aux_in[there, cols].astype(F32)
+            ) * (keep[c] * scale_grad)
+    polar_round(len(groups) - 1)
+    pol_ref[...] = pol_out[len(groups), pl.ds(half * a, half), pl.ds(0, naux)] * scale_pol
 
     info_copy.wait_send()
     for g in range(chunks):
@@ -387,7 +467,8 @@
             S_IN + g,
             twin,
         ).wait_send()
-    for copy in [up1, down1, up2, down2] + pair_copies + gpair + [gup2, gdown2, gup1, gdown1, gaux] + pol_copies:
+    sent = [up1, down1, up2, down2] + pair_copies + gup2 + gdown2 + gup1 + gdown1 + gaux
+    for copy in sent + [copy for group in gpair + pol_copies for copy in group]:
         copy.wait_send()
 
 
@@ -397,11 +478,11 @@
     naux = kern.shape[1]
     chunks = (B // 2) // ROWS
     tall = naux * ROWS
-    rounds = int(math.log2(nchain)) + 1
+    polars = 5 + 3 * (nchain >= 64) + (nchain >= 16)
+    rounds = 3 + (nchain >= 64) + (nchain >= 16)
     slabs = three_centre.reshape(half, B // ROWS, ROWS, W)
-    anyspace = pl.BlockSpec(memory_space=pl.ANY)
+    hbm = pl.BlockSpec(memory_space=pltpu.HBM)
     vmem = pl.BlockSpec(memory_space=pltpu.VMEM)
-    smem = pl.BlockSpec(memory_space=pltpu.SMEM)
     grad, pol = pl.pallas_call(
         functools.partial(
             kernel,
@@ -415,7 +496,7 @@
             jax.ShapeDtypeStruct((B // 2, W), F32),
             jax.ShapeDtypeStruct((half, naux), F32),
         ),
-        in_specs=[anyspace, anyspace, anyspace, vmem, smem, smem],
+        in_specs=[hbm] * 6,
         out_specs=(vmem, vmem),
         scratch_shapes=[
             pltpu.VMEM((chunks, naux, ROWS, W), BF16),
@@ -438,17 +519,20 @@
             pltpu.VMEM((2, B, 6 * B), BF16),
             pltpu.VMEM((2, B, 8 * B), BF16),
             pltpu.VMEM((2, B, 8 * B), BF16),
-            pltpu.VMEM((B, W), F32),
+            pltpu.VMEM((2, B // 2, W), F32),
             pltpu.VMEM((B // 2, W), BF16),
             pltpu.VMEM((B // 2, W), BF16),
             pltpu.VMEM((rounds + 1, naux, B), F32),
-            pltpu.VMEM((rounds, naux, B), F32),
-            pltpu.SemaphoreType.DMA((POLAR + rounds,)),
-            pltpu.SemaphoreType.DMA((POLAR + rounds,)),
-            pltpu.SemaphoreType.DMA((2 + chunks,)),
+            pltpu.VMEM((polars, naux, B), F32),
+            pltpu.VMEM((half, naux), BF16),
+            pltpu.SMEM((nchain,), jnp.int32),
+            pltpu.SMEM((half,), jnp.int32),
+            pltpu.SemaphoreType.DMA((POLAR + polars,)),
+            pltpu.SemaphoreType.DMA((POLAR + polars,)),
+            pltpu.SemaphoreType.DMA((5 + chunks,)),
         ],
         compiler_params=pltpu.CompilerParams(
-            collective_id=0, has_side_effects=True, vmem_limit_bytes=60 * 2**20
+            collective_id=0, has_side_effects=True, vmem_limit_bytes=VMEM_LIMIT
         ),
         name="rpa",
     )(occupied, virtual, slabs, kern, profile, atom_map)

time: 104 us -> 91.3 us (0.88)
  the two profiles are of different devices: /device:TPU:10 before, /device:TPU:1 now
where the time goes in v2:
time: 91.3 us; the launch traced here: 89.9 us
  Pallas kernels  86.3 us (95%)
  local copies, waits for them, and re-layouts  2.99 us (3%)
    pallas_call x1, Pallas kernels, body(): pl.pallas_call(functools.partial(kernel, nchain, naux, nchain // 4, 1.0 /...  86.3 us
    unnamed x2, local copies, waits for them, and re-layouts  2.99 us

profile of v2, /device:TPU:1, one launch (start us, length us, event | category | flops | bytes accessed | tf_op | source)
XLA Modules:
  0.0 89.9 jit_solution(9545833741833185827)
XLA Ops:
  0.6 86.3 %rpa.1 = (f32[64,1152]{1,0:T(8,128)}, f32[16,32]{1,0:T(8,128)}) custom-call(bf16[128,1152]{1,0:T(8,128)(2,1)} %occ_hbm.1, bf16[128,1152]{1,0:T(8,128)(2,1)} %vir_hbm.1, bf16[16,8,16,1152]{3,2,1,0:T(8,128)(2,1)} %bitcast.1, bf16[16,32]{1,0:T(8,128)(2,1)} %kern_hbm.1, s32[64]{0:T(128)} %profile_hbm.1, s32[16]{0:T(128)} %atom_hbm.1), custom_call_target="tpu_custom_call" | custom-call | tf_op jit(solution)/shard_map/rpa/pallas_call | solution.py:486
  86.9 1.7 %copy.10 = f32[64,1152]{1,0:T(8,128)} copy(f32[64,1152]{1,0:T(8,128)} %get-tuple-element.4) | data formatting | bytes 589824
  88.6 1.3 %copy.11 = f32[16,32]{1,0:T(8,128)} copy(f32[16,32]{1,0:T(8,128)} %get-tuple-element.5) | data formatting | bytes 4096

commit v3 on v2

--- a/solution.py
+++ b/solution.py
@@ -22,11 +22,10 @@
 PAIR = 8
 INFO = 12
 GPAIR = 13
-GUP2, GDOWN2, GUP1, GDOWN1, GAUX = 21, 23, 25, 27, 29
-POLAR = 31
 PIECES = 2
-RUN = B // 4
-VMEM_LIMIT = 60 * 2**20
+RUN = B // (2 * PIECES)
+GUP2, GDOWN2, GUP1, GDOWN1, GAUX, POLAR = [GPAIR + n * PIECES for n in (4, 5, 6, 7, 8, 9)]
+VMEM_LIMIT = 44 * 2**20
 
 
 def kernel(
@@ -102,12 +101,12 @@
                 device = device + size * (1 - 2 * lax.rem(lax.div(ci, size), 2))
         return (device, a)
 
-    groups = [[mate], [twin]]
+    groups = [[xor(1, v) for v in (1, 2, 3)]]
     if nchain >= 64:
         groups.append([xor(4, v) for v in (1, 2, 3)])
     if nchain >= 16:
         groups.append([xor(3, 1)])
-    groups.append([xor(1, v) for v in (1, 2, 3)])
+    groups += [[twin], [mate]]
     polar_peers = [device for group in groups for device in group]
 
     def remote(src, dst, number, device):
@@ -322,7 +321,7 @@
 
     def own_terms(p, run, d, cj, n=1):
         k = d + 4
-        return terms[pl.ds(k * B + run * 2 * RUN + p * RUN, RUN), pl.ds((cj + d) * B, n * B)] * keep[k]
+        return terms[pl.ds(k * B + run * (B // 2) + p * RUN, RUN), pl.ds((cj + d) * B, n * B)] * keep[k]
 
     def mates(p, run, slot, cj):
         return pair_in[slot, pl.ds((2 * p + run) * RUN, RUN), pl.ds(cj * B, B)].astype(F32)
@@ -345,6 +344,48 @@
             )
             gpair[p][q].start()
 
+    folded = jnp.where(same_row, gram[...], 0.0).reshape(naux, ROWS, tall).sum(1)
+    polar = jnp.dot(folded, pick, preferred_element_type=F32, precision=lax.Precision.HIGHEST)
+    square_row = lax.broadcasted_iota(jnp.int32, (naux, B), 0)
+    square_lane = lax.broadcasted_iota(jnp.int32, (naux, B), 1)
+    screen_lane = jnp.sum(jnp.where(square_row == square_lane, screen_all, 0.0), axis=0, keepdims=True)
+    polar = polar * screen_all * screen_lane
+    packed = polar[:8]
+    for n in range(1, naux // 8):
+        packed = packed + pltpu.roll(polar[8 * n : 8 * n + 8], n * naux, 1)
+    pol_out[0] = packed
+    pol_copies = []
+    for r, group in enumerate(groups):
+        first = sum(len(g) for g in groups[:r])
+        pol_copies.append(
+            [
+                remote(pol_out.at[r], pol_in.at[first + n], POLAR + first + n, device)
+                for n, device in enumerate(group)
+            ]
+        )
+
+    def polar_start(r):
+        for copy in pol_copies[r]:
+            copy.start()
+
+    def polar_round(r):
+        for copy in pol_copies[r]:
+            copy.wait_recv()
+        first = sum(len(g) for g in groups[:r])
+        value = pol_out[r] + pol_in[first]
+        if len(groups[r]) == 3:
+            value = value + (pol_in[first + 1] + pol_in[first + 2])
+        pol_out[r + 1] = value
+        if r + 1 < len(groups):
+            polar_start(r + 1)
+
+    ahead = list(range(len(groups) - 1))
+
+    def advance():
+        if ahead:
+            polar_round(ahead.pop(0))
+
+    polar_start(0)
     gup2, gdown2, gup1, gdown1, gaux = [], [], [], [], []
     for p in range(PIECES):
         for q in (0, 3, 1, 2):
@@ -368,39 +409,7 @@
         gdown2.append(remote(out2.at[1, piece(p)], in2.at[1, piece(p)], GDOWN2 + p, down))
         gdown2[p].start()
 
-    folded = jnp.where(same_row, gram[...], 0.0).reshape(naux, ROWS, tall).sum(1)
-    polar = jnp.dot(folded, pick, preferred_element_type=F32, precision=lax.Precision.HIGHEST)
-    square_row = lax.broadcasted_iota(jnp.int32, (naux, B), 0)
-    square_lane = lax.broadcasted_iota(jnp.int32, (naux, B), 1)
-    screen_lane = jnp.sum(jnp.where(square_row == square_lane, screen_all, 0.0), axis=0, keepdims=True)
-    pol_out[0] = polar * screen_all * screen_lane
-    pol_copies = []
-    for r, group in enumerate(groups):
-        first = sum(len(g) for g in groups[:r])
-        pol_copies.append(
-            [
-                remote(pol_out.at[r], pol_in.at[first + n], POLAR + first + n, device)
-                for n, device in enumerate(group)
-            ]
-        )
-
-    def polar_start(r):
-        for copy in pol_copies[r]:
-            copy.start()
-
-    def polar_round(r):
-        for copy in pol_copies[r]:
-            copy.wait_recv()
-        first = sum(len(g) for g in groups[:r])
-        value = pol_out[r] + pol_in[first]
-        if len(groups[r]) == 3:
-            value = value + (pol_in[first + 1] + pol_in[first + 2])
-        pol_out[r + 1] = value
-        if r + 1 < len(groups):
-            polar_start(r + 1)
-
-    polar_start(0)
-    polar_round(0)
+    advance()
     for p in range(PIECES):
         gup2[p].wait_recv()
         for run in (0, 1):
@@ -426,8 +435,7 @@
                 out1[1, at, pl.ds(c * B, B)] = part.astype(BF16)
         gdown1.append(remote(out1.at[1, piece(p)], in1.at[1, piece(p)], GDOWN1 + p, down))
         gdown1[p].start()
-        if p + 1 < len(groups) - 1:
-            polar_round(p + 1)
+        advance()
     for p in range(PIECES):
         gup1[p].wait_recv()
         gdown1[p].wait_recv()
@@ -444,10 +452,7 @@
         aux_out[there, :] = total[1 - a, there, :].astype(BF16)
         gaux.append(remote(aux_out.at[there], aux_in.at[there], GAUX + p, twin))
         gaux[p].start()
-        if p + PIECES + 1 < len(groups) - 1:
-            polar_round(p + PIECES + 1)
-    for r in range(min(2 * PIECES + 1, len(groups) - 1), len(groups) - 1):
-        polar_round(r)
+        advance()
     for p in range(PIECES):
         gaux[p].wait_recv()
         there = pl.ds(p * RUN, RUN)
@@ -457,7 +462,10 @@
                 total[a, there, cols] + aux_in[there, cols].astype(F32)
             ) * (keep[c] * scale_grad)
     polar_round(len(groups) - 1)
-    pol_ref[...] = pol_out[len(groups), pl.ds(half * a, half), pl.ds(0, naux)] * scale_pol
+    packed = pol_out[len(groups)] * scale_pol
+    for n in range(half // 8):
+        here = [pltpu.roll(packed, (B - (n + slab * half // 8) * naux) % B, 1) for slab in (0, 1)]
+        pol_ref[pl.ds(8 * n, 8), :] = jnp.where(a == 0, here[0], here[1])[:, :naux]
 
     info_copy.wait_send()
     for g in range(chunks):
@@ -522,8 +530,8 @@
             pltpu.VMEM((2, B // 2, W), F32),
             pltpu.VMEM((B // 2, W), BF16),
             pltpu.VMEM((B // 2, W), BF16),
-            pltpu.VMEM((rounds + 1, naux, B), F32),
-            pltpu.VMEM((polars, naux, B), F32),
+            pltpu.VMEM((rounds + 1, 8, B), F32),
+            pltpu.VMEM((polars, 8, B), F32),
             pltpu.VMEM((half, naux), BF16),
             pltpu.SMEM((nchain,), jnp.int32),
             pltpu.SMEM((half,), jnp.int32),
@@ -535,7 +543,7 @@
             collective_id=0, has_side_effects=True, vmem_limit_bytes=VMEM_LIMIT
         ),
         name="rpa",
-    )(occupied, virtual, slabs, kern, profile, atom_map)
+    )(*[pltpu.with_memory_space_constraint(x, pltpu.HBM) for x in (occupied, virtual, slabs, kern, profile, atom_map)])
     return grad, pol
 
 

time: 91.3 us -> 89.1 us (0.976)
  the two profiles are of different devices: /device:TPU:1 before, /device:TPU:60 now
where the time goes in v3:
time: 89.1 us; the launch traced here: 89 us
  Pallas kernels  87.1 us (98%)
  local copies, waits for them, and re-layouts  1.31 us (1%)
    pallas_call x1, Pallas kernels, body(): pl.pallas_call(functools.partial(kernel, nchain, naux, nchain // 4, 1.0 /...  87.1 us

profile of v3, /device:TPU:60, one launch (start us, length us, event | category | flops | bytes accessed | tf_op | source)
XLA Modules:
  0.0 89.0 jit_solution(14125155198400292276)
XLA Ops:
  0.6 87.1 %rpa.1 = (f32[64,1152]{1,0:T(8,128)S(1)}, f32[16,32]{1,0:T(8,128)S(1)}) custom-call(bf16[128,1152]{1,0:T(8,128)(2,1)} %occ_hbm.1, bf16[128,1152]{1,0:T(8,128)(2,1)} %vir_hbm.1, bf16[16,8,16,1152]{3,2,1,0:T(8,128)(2,1)} %bitcast.1, bf16[16,32]{1,0:T(8,128)(2,1)} %kern_hbm.1, s32[64]{0:T(128)} %profile_hbm.1, s32[16]{0:T(128)} %atom_hbm.1), custom_call_target="tpu_custom_call" | custom-call | tf_op jit(solution)/shard_map/rpa/pallas_call | solution.py:494
  87.7 0.7 copy.10
  88.4 0.6 copy.11

commit v4 on v3

--- a/solution.py
+++ b/solution.py
@@ -24,7 +24,7 @@
 GPAIR = 13
 PIECES = 2
 RUN = B // (2 * PIECES)
-GUP2, GDOWN2, GUP1, GDOWN1, GAUX, POLAR = [GPAIR + n * PIECES for n in (4, 5, 6, 7, 8, 9)]
+GUP2, GDOWN2, GUP1, GDOWN1, GAUX, POLAR = [GPAIR + n * PIECES for n in (4, 5, 6, 8, 10, 11)]
 VMEM_LIMIT = 44 * 2**20
 
 
@@ -86,6 +86,8 @@
     flip_down = 1 - lax.div(inrow + 3, 4)
     up = (2 * lax.rem(chip + 1, chips) + core, lax.rem(a + flip_up, 2))
     down = (2 * lax.rem(chip + chips - 1, chips) + core, lax.rem(a + flip_down, 2))
+    up_twin = (up[0], 1 - up[1])
+    down_twin = (down[0], 1 - down[1])
     mate = (2 * chip + 1 - core, a)
     twin = (ci, 1 - a)
 
@@ -101,12 +103,12 @@
                 device = device + size * (1 - 2 * lax.rem(lax.div(ci, size), 2))
         return (device, a)
 
-    groups = [[xor(1, v) for v in (1, 2, 3)]]
+    groups = [[xor(1, v) for v in (1, 2, 3)], [twin]]
     if nchain >= 64:
         groups.append([xor(4, v) for v in (1, 2, 3)])
     if nchain >= 16:
         groups.append([xor(3, 1)])
-    groups += [[twin], [mate]]
+    groups += [[mate]]
     polar_peers = [device for group in groups for device in group]
 
     def remote(src, dst, number, device):
@@ -140,7 +142,7 @@
         pair_in[slot, :, pl.ds(c0 * B, n * B)] = jnp.zeros((B, n * B), BF16)
 
     barrier = pltpu.get_barrier_semaphore()
-    greeted = [up, down] + polar_peers
+    greeted = [up, down, up_twin, down_twin] + polar_peers
     for device in greeted:
         pl.semaphore_signal(barrier, inc=1, device_id=device, device_id_type=MESH)
     for copy in own_copies + table_copies + slab_copies:
@@ -410,6 +412,24 @@
         gdown2[p].start()
 
     advance()
+
+    for p in range(PIECES):
+        for run in (0, 1):
+            for c in range(SLOTS):
+                total[run, pl.ds(p * RUN, RUN), pl.ds(c * B, B)] = mates(p, run, 2, c) + own_terms(p, run, 0, c)
+    aux_out[...] = total[1 - a].astype(BF16)
+    gaux.append(remote(aux_out, aux_in, GAUX, twin))
+    gaux[0].start()
+
+    def last_hop(way, number, p, near, far):
+        copies = []
+        for kind, device in enumerate((near, far)):
+            copies.append(
+                remote(out1.at[way, p, device[1]], in1.at[way, kind, p], number + 2 * p + kind, device)
+            )
+            copies[kind].start()
+        return copies
+
     for p in range(PIECES):
         gup2[p].wait_recv()
         for run in (0, 1):
@@ -420,9 +440,8 @@
                     part = part + own_terms(p, run, 2, c)
                 if c < 6:
                     part = part + in2[0, at, pl.ds(c * B, B)].astype(F32)
-                out1[0, at, pl.ds(c * B, B)] = part.astype(BF16)
-        gup1.append(remote(out1.at[0, piece(p)], in1.at[0, piece(p)], GUP1 + p, up))
-        gup1[p].start()
+                out1[0, p, run, :, pl.ds(c * B, B)] = part.astype(BF16)
+        gup1.append(last_hop(0, GUP1, p, up, up_twin))
         gdown2[p].wait_recv()
         for run in (0, 1):
             at = pl.ds((2 * p + run) * RUN, RUN)
@@ -432,35 +451,25 @@
                     part = part + own_terms(p, run, -2, c + 1)
                 if c >= 2:
                     part = part + in2[1, at, pl.ds((c - 2) * B, B)].astype(F32)
-                out1[1, at, pl.ds(c * B, B)] = part.astype(BF16)
-        gdown1.append(remote(out1.at[1, piece(p)], in1.at[1, piece(p)], GDOWN1 + p, down))
-        gdown1[p].start()
+                out1[1, p, run, :, pl.ds(c * B, B)] = part.astype(BF16)
+        gdown1.append(last_hop(1, GDOWN1, p, down, down_twin))
         advance()
+    while ahead:
+        advance()
+    gaux[0].wait_recv()
     for p in range(PIECES):
-        gup1[p].wait_recv()
-        gdown1[p].wait_recv()
-        for run in (0, 1):
-            at = pl.ds((2 * p + run) * RUN, RUN)
-            for c in range(SLOTS):
-                part = mates(p, run, 2, c) + own_terms(p, run, 0, c)
-                if c < 8:
-                    part = part + in1[0, at, pl.ds(c * B, B)].astype(F32)
-                if c >= 1:
-                    part = part + in1[1, at, pl.ds((c - 1) * B, B)].astype(F32)
-                total[run, pl.ds(p * RUN, RUN), pl.ds(c * B, B)] = part
-        there = pl.ds(p * RUN, RUN)
-        aux_out[there, :] = total[1 - a, there, :].astype(BF16)
-        gaux.append(remote(aux_out.at[there], aux_in.at[there], GAUX + p, twin))
-        gaux[p].start()
-        advance()
-    for p in range(PIECES):
-        gaux[p].wait_recv()
+        for copy in gup1[p] + gdown1[p]:
+            copy.wait_recv()
         there = pl.ds(p * RUN, RUN)
         for c in range(SLOTS):
             cols = pl.ds(c * B, B)
-            grad_ref[there, cols] = (
-                total[a, there, cols] + aux_in[there, cols].astype(F32)
-            ) * (keep[c] * scale_grad)
+            part = total[a, there, cols] + aux_in[there, cols].astype(F32)
+            for kind in (0, 1):
+                if c < 8:
+                    part = part + in1[0, kind, p, :, cols].astype(F32)
+                if c >= 1:
+                    part = part + in1[1, kind, p, :, pl.ds((c - 1) * B, B)].astype(F32)
+            grad_ref[there, cols] = part * (keep[c] * scale_grad)
     polar_round(len(groups) - 1)
     packed = pol_out[len(groups)] * scale_pol
     for n in range(half // 8):
@@ -475,8 +484,8 @@
             S_IN + g,
             twin,
         ).wait_send()
-    sent = [up1, down1, up2, down2] + pair_copies + gup2 + gdown2 + gup1 + gdown1 + gaux
-    for copy in sent + [copy for group in gpair + pol_copies for copy in group]:
+    sent = [up1, down1, up2, down2] + pair_copies + gup2 + gdown2 + gaux
+    for copy in sent + [copy for group in gpair + gup1 + gdown1 + pol_copies for copy in group]:
         copy.wait_send()
 
 
@@ -525,8 +534,8 @@
             pltpu.VMEM((5, B, W), BF16),
             pltpu.VMEM((2, B, 6 * B), BF16),
             pltpu.VMEM((2, B, 6 * B), BF16),
-            pltpu.VMEM((2, B, 8 * B), BF16),
-            pltpu.VMEM((2, B, 8 * B), BF16),
+            pltpu.VMEM((2, PIECES, 2, RUN, 8 * B), BF16),
+            pltpu.VMEM((2, 2, PIECES, RUN, 8 * B), BF16),
             pltpu.VMEM((2, B // 2, W), F32),
             pltpu.VMEM((B // 2, W), BF16),
             pltpu.VMEM((B // 2, W), BF16),

time: 89.1 us -> 85.7 us (0.962)
  the two profiles are of different devices: /device:TPU:60 before, /device:TPU:1 now
where the time goes in v4:
time: 85.7 us; the launch traced here: 85.5 us
  Pallas kernels  83.6 us (98%)
  local copies, waits for them, and re-layouts  1.31 us (2%)
    pallas_call x1, Pallas kernels, body(): pl.pallas_call(functools.partial(kernel, nchain, naux, nchain // 4, 1.0 /...  83.6 us

profile of v4, /device:TPU:1, one launch (start us, length us, event | category | flops | bytes accessed | tf_op | source)
XLA Modules:
  0.0 85.5 jit_solution(14269078140728796662)
XLA Ops:
  0.6 83.6 %rpa.1 = (f32[64,1152]{1,0:T(8,128)S(1)}, f32[16,32]{1,0:T(8,128)S(1)}) custom-call(bf16[128,1152]{1,0:T(8,128)(2,1)} %occ_hbm.1, bf16[128,1152]{1,0:T(8,128)(2,1)} %vir_hbm.1, bf16[16,8,16,1152]{3,2,1,0:T(8,128)(2,1)} %bitcast.1, bf16[16,32]{1,0:T(8,128)(2,1)} %kern_hbm.1, s32[64]{0:T(128)} %profile_hbm.1, s32[16]{0:T(128)} %atom_hbm.1), custom_call_target="tpu_custom_call" | custom-call | tf_op jit(solution)/shard_map/rpa/pallas_call | solution.py:503
  84.2 0.7 copy.10
  84.9 0.6 copy.11

commit v5 on v4

--- a/solution.py
+++ b/solution.py
@@ -121,6 +121,26 @@
             device_id_type=MESH,
         )
 
+    class PerCore:
+        def __init__(self, src, dst, number, device, spans):
+            self.copies = [
+                remote(src.at[:, pl.ds(c0 * B, n * B)], dst.at[:, pl.ds(c0 * B, n * B)], number, device)
+                for c0, n in spans
+            ]
+
+        def each(self, act):
+            for which, copy in enumerate(self.copies):
+                pl.when(core == which)(functools.partial(act, copy))
+
+        def start(self):
+            self.each(lambda copy: copy.start())
+
+        def wait_recv(self):
+            self.each(lambda copy: copy.wait_recv())
+
+        def wait_send(self):
+            self.each(lambda copy: copy.wait_send())
+
     own_copies = [
         pltpu.make_async_copy(occ_hbm, halo.at[2, 0], local_sem.at[0]),
         pltpu.make_async_copy(vir_hbm, halo.at[2, 1], local_sem.at[1]),
@@ -141,12 +161,28 @@
     for slot, c0, n in ((0, 3, 6), (1, 1, 2), (2, 0, 1), (2, 8, 1), (3, 6, 2), (4, 0, 6)):
         pair_in[slot, :, pl.ds(c0 * B, n * B)] = jnp.zeros((B, n * B), BF16)
 
+    in2[0, :, pl.ds(5 * B, B)] = jnp.zeros((B, B), BF16)
+    in2[1, :, pl.ds(0, B)] = jnp.zeros((B, B), BF16)
+    in1[0, :, :, :, pl.ds(7 * B, B)] = jnp.zeros((2, PIECES, RUN, B), BF16)
+    in1[1, :, :, :, pl.ds(0, B)] = jnp.zeros((2, PIECES, RUN, B), BF16)
+
     barrier = pltpu.get_barrier_semaphore()
     greeted = [up, down, up_twin, down_twin] + polar_peers
     for device in greeted:
         pl.semaphore_signal(barrier, inc=1, device_id=device, device_id_type=MESH)
     for copy in own_copies + table_copies + slab_copies:
         copy.start()
+    pl.semaphore_wait(barrier, len(greeted))
+
+    def slab_out(g):
+        return remote(
+            tc_hbm.at[:, chunks * (1 - a) + g],
+            s_buf.at[g, pl.ds(half * a, half)],
+            S_IN + g,
+            twin,
+        )
+
+    slab_out(0).start()
     for copy in table_copies:
         copy.wait()
     row_id = lax.broadcasted_iota(jnp.int32, (half, B), 0)
@@ -157,18 +193,10 @@
     info[a, 0] = jnp.zeros((half, B), F32)
     info[a, 0, :, pl.ds(0, naux)] = kern_ref[...].astype(F32)
     info[a, 1] = screen
-    pl.semaphore_wait(barrier, len(greeted))
-
     info_copy = remote(info.at[a], info.at[a], INFO, twin)
-    for g in range(chunks):
-        remote(
-            tc_hbm.at[:, chunks * (1 - a) + g],
-            s_buf.at[g, pl.ds(half * a, half)],
-            S_IN + g,
-            twin,
-        ).start()
-        if g == 0:
-            info_copy.start()
+    info_copy.start()
+    for g in range(1, chunks):
+        slab_out(g).start()
     for copy in own_copies:
         copy.wait()
     up1 = remote(halo.at[2, :, :, pl.ds(B, 8 * B)], halo.at[1, :, :, pl.ds(B, 8 * B)], UP1, up)
@@ -399,7 +427,7 @@
                 if c < 5:
                     part = part + own_terms(p, run, 4, c)
                 out2[0, at, pl.ds(c * B, B)] = part.astype(BF16)
-        gup2.append(remote(out2.at[0, piece(p)], in2.at[0, piece(p)], GUP2 + p, up))
+        gup2.append(PerCore(out2.at[0, piece(p)], in2.at[0, piece(p)], GUP2 + p, up, ((0, 6), (0, 5))))
         gup2[p].start()
         for run in (0, 1):
             at = pl.ds((2 * p + run) * RUN, RUN)
@@ -408,7 +436,7 @@
                 if c >= 1:
                     part = part + own_terms(p, run, -4, c + 3)
                 out2[1, at, pl.ds(c * B, B)] = part.astype(BF16)
-        gdown2.append(remote(out2.at[1, piece(p)], in2.at[1, piece(p)], GDOWN2 + p, down))
+        gdown2.append(PerCore(out2.at[1, piece(p)], in2.at[1, piece(p)], GDOWN2 + p, down, ((1, 5), (0, 6))))
         gdown2[p].start()
 
     advance()
@@ -425,7 +453,13 @@
         copies = []
         for kind, device in enumerate((near, far)):
             copies.append(
-                remote(out1.at[way, p, device[1]], in1.at[way, kind, p], number + 2 * p + kind, device)
+                PerCore(
+                    out1.at[way, p, device[1]],
+                    in1.at[way, kind, p],
+                    number + 2 * p + kind,
+                    device,
+                    (((0, 8), (0, 7)), ((1, 7), (0, 8)))[way],
+                )
             )
             copies[kind].start()
         return copies
@@ -478,12 +512,7 @@
 
     info_copy.wait_send()
     for g in range(chunks):
-        remote(
-            tc_hbm.at[:, chunks * (1 - a) + g],
-            s_buf.at[g, pl.ds(half * a, half)],
-            S_IN + g,
-            twin,
-        ).wait_send()
+        slab_out(g).wait_send()
     sent = [up1, down1, up2, down2] + pair_copies + gup2 + gdown2 + gaux
     for copy in sent + [copy for group in gpair + gup1 + gdown1 + pol_copies for copy in group]:
         copy.wait_send()

time: 85.7 us -> 85.4 us (level)
  no operation moved by 1% of the time
where the time goes in v5:
time: 85.4 us; the launch traced here: 85.3 us
  Pallas kernels  83.3 us (98%)
  local copies, waits for them, and re-layouts  1.31 us (2%)
    pallas_call x1, Pallas kernels, body(): pl.pallas_call(functools.partial(kernel, nchain, naux, nchain // 4, 1.0 /...  83.3 us

profile of v5, /device:TPU:1, one launch (start us, length us, event | category | flops | bytes accessed | tf_op | source)
XLA Modules:
  0.0 85.3 jit_solution(11927349540657694255)
XLA Ops:
  0.6 83.3 %rpa.1 = (f32[64,1152]{1,0:T(8,128)S(1)}, f32[16,32]{1,0:T(8,128)S(1)}) custom-call(bf16[128,1152]{1,0:T(8,128)(2,1)} %occ_hbm.1, bf16[128,1152]{1,0:T(8,128)(2,1)} %vir_hbm.1, bf16[16,8,16,1152]{3,2,1,0:T(8,128)(2,1)} %bitcast.1, bf16[16,32]{1,0:T(8,128)(2,1)} %kern_hbm.1, s32[64]{0:T(128)} %profile_hbm.1, s32[16]{0:T(128)} %atom_hbm.1), custom_call_target="tpu_custom_call" | custom-call | tf_op jit(solution)/shard_map/rpa/pallas_call | solution.py:532
  84.0 0.7 copy.10
  84.7 0.6 copy.11
